TPU v7x, 32 devices: a whole 2x2x4 slice. The times are simulated.
32 devices in a mesh: groups: 2 (over x), blk: 8 (over z, y), rep: 2 (over core).
Axes of the slice: x: 2, y: 2, z: 4, core: 2. Of those that a mesh axis runs over, the one named last changes fastest.
Arguments:
- resident: bfloat16 [32768, 768], P(('groups', 'blk', 'rep')), parts along dimension 0, may hold values from -600 to 600
- ingest: bfloat16 [16384, 768], P(('groups', 'blk', 'rep')), parts along dimension 0, may hold values from -600 to 600
- cluster_ids: int32 [16384], P(('groups', 'blk', 'rep')), parts along dimension 0, may hold values from 0 to 127, as said below
Outputs:
- resident_score: float32 [32768], P(('groups', 'blk', 'rep')), parts along dimension 0
- ingest_score: float32 [16384], P(('groups', 'blk', 'rep')), parts along dimension 0
There are 2 independent parts, one for each index of `groups`. A program takes and returns all parts, laid end to end along the dimension named above; each array names one. Nothing has to cross between parts.
Inputs may be any that keep to these rules, and one draw needn't show every extreme that they name: `cluster_ids`: clusters 16 * p to 16 * p + 15 belong to cycle position p. At most 96 documents of one device belong to one cycle position, and in every draw some cycle position receives 96 from every device.
All inputs are finite; a program needn't handle non-finite values.
Results may differ from a plain program's by a relative error of at most 0.0003.
Values may be sent and summed in bfloat16 or wider, within the bound.
No kernel may reach another device: no remote copies, remote signals or barrier semaphores. Data moves between devices by JAX's collectives and lax.ppermute only.
A program may use at most 64 MiB of HBM per device.

v0:
```python
import jax
import jax.numpy as jnp
from jax import lax
from jax.sharding import PartitionSpec as P

INGEST_DEV = 512
CL_OWN = 16
CYCLE_STEPS = 4


temper = 0.2
epsilon = 1e-06


def shifted(value, axis, steps):
    count = lax.axis_size(axis)
    pairs = [(source, (source + steps) % count) for source in range(count)]
    return lax.ppermute(value, axis, pairs)


def unit_rows(rows):
    values = rows.astype(jnp.float32)
    squares = jnp.sum(values * values, axis=-1, keepdims=True) + epsilon
    factor = lax.rsqrt(squares)
    return (values * factor).astype(jnp.bfloat16)


def kernel_sums(visitors, occupancy, residents):
    count_rows = visitors.shape[0]
    block_rows = 512
    num_blocks = count_rows // block_rows
    visit_blocks = visitors.reshape(num_blocks, block_rows, visitors.shape[1])
    live_blocks = occupancy.astype(jnp.float32).reshape(num_blocks, block_rows)

    def tile_sums(running, pieces):
        visit_tile, live_tile = pieces
        scores = jnp.einsum("vd,rd->vr", visit_tile, residents, preferred_element_type=jnp.float32)
        kernel = jnp.exp((scores - 1.0) / temper)
        return (running + jnp.sum(kernel * live_tile[:, None], axis=0), jnp.sum(kernel, axis=1))

    resident_part, visit_parts = lax.scan(
        tile_sums, jnp.zeros((residents.shape[0],), jnp.float32), (visit_blocks, live_blocks)
    )
    return (visit_parts.reshape(count_rows), resident_part)


def on_device(resident, ingest, cluster_ids):
    cycle_size = lax.axis_size("blk")
    slot_count = 3 * INGEST_DEV // (2 * cycle_size)
    columns = ingest.shape[1]
    owners = cluster_ids // CL_OWN
    onehot = (owners[:, None] == jnp.arange(cycle_size, dtype=jnp.int32)[None, :]).astype(jnp.int32)
    rank_within = jnp.sum((jnp.cumsum(onehot, axis=0) - onehot) * onehot, axis=1)
    targets = owners * slot_count + rank_within
    unit_ingest = unit_rows(ingest)
    outgoing = (
        jnp.zeros((cycle_size * slot_count, columns), jnp.bfloat16).at[targets].set(unit_ingest)
    )
    filled = (
        jnp.zeros((cycle_size * slot_count,), jnp.bfloat16)
        .at[targets]
        .set(jnp.ones((ingest.shape[0],), jnp.bfloat16))
    )
    arrived, present = (
        lax.all_to_all(
            outgoing.reshape(cycle_size, slot_count, columns),
            "blk",
            split_axis=0,
            concat_axis=0,
            tiled=True,
        ),
        lax.all_to_all(
            filled.reshape(cycle_size, slot_count), "blk", split_axis=0, concat_axis=0, tiled=True
        ),
    )
    visitors, marked = (
        lax.all_gather(
            arrived.reshape(cycle_size * slot_count, columns), "rep", axis=0, tiled=True
        ),
        lax.all_gather(present.reshape(cycle_size * slot_count), "rep", axis=0, tiled=True),
    )
    unit_resident = unit_rows(resident)
    visit_total = jnp.zeros((visitors.shape[0],), jnp.float32)
    resident_total = jnp.zeros((resident.shape[0],), jnp.float32)
    moving = unit_resident
    for rotation in range(CYCLE_STEPS + 1):
        if rotation > 0:
            moving = shifted(moving, "blk", -1)
            resident_total = shifted(resident_total, "blk", -1)
        visit_part, resident_part = kernel_sums(visitors, marked, moving)
        visit_total = visit_total + visit_part
        resident_total = resident_total + resident_part
    resident_total = shifted(resident_total, "blk", CYCLE_STEPS)
    own_sums = lax.psum_scatter(visit_total, "rep", scatter_dimension=0, tiled=True)
    returned = lax.all_to_all(
        own_sums.reshape(cycle_size, slot_count), "blk", split_axis=0, concat_axis=0, tiled=True
    )
    density = returned.reshape(cycle_size * slot_count)[targets]
    return (jnp.log1p(resident_total), jnp.log1p(density))


def solution(mesh):
    in_specs = (
        P(("groups", "blk", "rep"), None),
        P(("groups", "blk", "rep"), None),
        P(("groups", "blk", "rep")),
    )
    out_specs = (P(("groups", "blk", "rep")), P(("groups", "blk", "rep")))
    return jax.shard_map(
        on_device, mesh=mesh, in_specs=in_specs, out_specs=out_specs, check_vma=False
    )
```

profile of v0, /device:TPU:0, one launch (start us, length us, event | category | flops | bytes accessed | tf_op | source)
XLA Modules:
  0.0 246.6 jit_solution(1169639654223723003)
XLA Ops:
  7.2 0.7 fusion.45
  7.9 0.7 add_select_fusion
  8.6 1.1 reduce-window.6
  10.0 0.7 compare_select_fusion
  10.7 1.4 fusion.27
  12.1 4.4 %scatter_custom_fusion = bf16[768,768]{1,0:T(8,128)(2,1)} fusion(s32[512]{0:T(512)S(1)} %compare_select_fusion, bf16[512,768]{1,0:T(8,128)(2,1)} %param.14, f32[512]{0:T(512)S(1)} %add_rsqrt_fusion.1, bf16[]{:T(256)} %constant.197.clone.1), kind=kCustom, calls=%fused_computation.56 | custom fusion | flops 1179648 | bytes 1968130 | tf_op jit(solution)/shard_map/scatter | solution.py:57
  16.5 7.3 %all-to-all-start = ((bf16[8,96,768]{2,1,0:T(8,128)(2,1)}), bf16[8,96,768]{2,1,0:T(8,128)(2,1)S(1)}, u32[]{:S(2)}, u32[]{:S(2)}) async-start(bf16[8,96,768]{2,1,0:T(8,128)(2,1)} %bitcast.3), calls=%async_computation | async-start | bytes 2359296 | tf_op jit(solution)/shard_map/all_to_all | solution.py:65
  24.2 1.5 fusion.26
  25.8 4.7 %collective-permute-start.1 = (bf16[1024,768]{1,0:T(8,128)(2,1)}, bf16[1024,768]{1,0:T(8,128)(2,1)}, u32[]{:S(2)}, u32[]{:S(2)}) collective-permute-start(bf16[1024,768]{1,0:T(8,128)(2,1)} %fusion.26), channel_id=1, source_target_pairs={{0,14},{2,0},{4,2},{6,4},{8,6},{10,8},{12,10},{14,12},{1,15},{3,1}... | collective-permute-start | bytes 4718600 | tf_op jit(solution)/shard_map/ppermute | solution.py:18
  30.4 23.3 %all-to-all-done = bf16[8,96,768]{2,1,0:T(8,128)(2,1)S(1)} async-done(((bf16[8,96,768]{2,1,0:T(8,128)(2,1)}), bf16[8,96,768]{2,1,0:T(8,128)(2,1)S(1)}, u32[]{:S(2)}, u32[]{:S(2)}) %all-to-all-start) | async-done | bytes 1179680 | tf_op jit(solution)/shard_map/all_to_all | solution.py:65
  53.8 1.1 copy-done.1
  54.9 22.2 %collective-permute-done.1 = bf16[1024,768]{1,0:T(8,128)(2,1)} collective-permute-done((bf16[1024,768]{1,0:T(8,128)(2,1)}, bf16[1024,768]{1,0:T(8,128)(2,1)}, u32[]{:S(2)}, u32[]{:S(2)}) %collective-permute-start.1) | collective-permute-done | bytes 1572896 | tf_op jit(solution)/shard_map/ppermute | solution.py:18
  77.1 9.4 %collective-permute-start.3 = (bf16[1024,768]{1,0:T(8,128)(2,1)}, bf16[1024,768]{1,0:T(8,128)(2,1)}, u32[]{:S(2)}, u32[]{:S(2)}) collective-permute-start(bf16[1024,768]{1,0:T(8,128)(2,1)} %collective-permute-done.1), channel_id=1, source_target_pairs={{0,14},{2,0},{4,2},{6,4},{8,6},{10,8},{12,10},{14,12},{1,15},{3,1}... | collective-permute-start | bytes 4718600 | tf_op jit(solution)/shard_map/ppermute | solution.py:18
  86.6 3.8 %scatter_custom_fusion.1 = bf16[768]{0:T(1024)(128)(2,1)S(1)} fusion(s32[512]{0:T(512)S(1)} %compare_select_fusion, bf16[512]{0:T(512)(128)(2,1)S(1)} %broadcast.118, bf16[]{:T(256)} %constant.197.clone.1), kind=kCustom, calls=%fused_computation.79 | custom fusion | bytes 1538 | tf_op jit(solution)/shard_map/scatter | solution.py:62
  90.4 0.7 all_to_all.20
  91.0 4.9 %all-to-all-start.1 = ((bf16[8,1,96]{2,1,0:T(2,128)(2,1)}), bf16[8,1,96]{2,1,0:T(2,128)(2,1)S(1)}, u32[]{:S(2)}, u32[]{:S(2)}) async-start(bf16[8,1,96]{2,1,0:T(2,128)(2,1)} %all_to_all.20), calls=%async_computation.1 | async-start | bytes 8192 | tf_op jit(solution)/shard_map/all_to_all | solution.py:72
  97.1 26.5 %all-to-all-done.1 = bf16[8,1,96]{2,1,0:T(2,128)(2,1)S(1)} async-done(((bf16[8,1,96]{2,1,0:T(2,128)(2,1)}), bf16[8,1,96]{2,1,0:T(2,128)(2,1)S(1)}, u32[]{:S(2)}, u32[]{:S(2)}) %all-to-all-start.1) | async-done | bytes 1568 | tf_op jit(solution)/shard_map/all_to_all | solution.py:72
  123.7 1.8 all-gather
  125.6 2.3 collective-permute-start.5
  127.9 8.9 %while.75 = (s32[]{:T(128)}, f32[1024]{0:T(1024)S(1)}, f32[3,512]{1,0:T(4,128)S(1)}, bf16[3,512,768]{2,1,0:T(8,128)(2,1)}, bf16[1024,768]{1,0:T(8,128)(2,1)}, /*index=5*/f32[3,512]{1,0:T(4,128)S(1)}, s32[]{:T(128)}, s32[]{:T(128)}) while((s32[]{:T(128)}, f32[1024]{0:T(1024)S(1)}, f32[3,512]{1,0:T(4,128)S(1)}, ...), condition=%wide.region_10.11_spmd.clone, body=%wide.region_7.10_spmd.clone.sunk | while | flops 807928320 | bytes 2388083 | solution.py:41
  127.9 2.9 %fusion.57 = (f32[512]{0:T(512)S(1)}, f32[1024]{0:T(1024)S(1)}) fusion(f32[512]{0:T(512)S(1)} %bitcast.100, bf16[1024,768]{1,0:T(8,128)(2,1)} %get-tuple-element.802, bf16[3,512,768]{2,1,0:T(8,128)(2,1)} %get-tuple-element.801, s32[]{:T(128)S(6)} %copy.14), kind=kOutput, calls=%fused_computation.5.clone.1 | convolution fusion | flops 807926272 | bytes 2367492 | tf_op jit(solution)/shard_map/while/body/eval_jaxpr/vd,rd->vr/dot_general | solution.py:37
  130.9 2.9 %fusion.57 = (f32[512]{0:T(512)S(1)}, f32[1024]{0:T(1024)S(1)}) fusion(f32[512]{0:T(512)S(1)} %bitcast.100, bf16[1024,768]{1,0:T(8,128)(2,1)} %get-tuple-element.802, bf16[3,512,768]{2,1,0:T(8,128)(2,1)} %get-tuple-element.801, s32[]{:T(128)S(6)} %copy.14), kind=kOutput, calls=%fused_computation.5.clone.1 | convolution fusion | flops 807926272 | bytes 2367492 | tf_op jit(solution)/shard_map/while/body/eval_jaxpr/vd,rd->vr/dot_general | solution.py:37
  133.9 2.9 %fusion.57 = (f32[512]{0:T(512)S(1)}, f32[1024]{0:T(1024)S(1)}) fusion(f32[512]{0:T(512)S(1)} %bitcast.100, bf16[1024,768]{1,0:T(8,128)(2,1)} %get-tuple-element.802, bf16[3,512,768]{2,1,0:T(8,128)(2,1)} %get-tuple-element.801, s32[]{:T(128)S(6)} %copy.14), kind=kOutput, calls=%fused_computation.5.clone.1 | convolution fusion | flops 807926272 | bytes 2367492 | tf_op jit(solution)/shard_map/while/body/eval_jaxpr/vd,rd->vr/dot_general | solution.py:37
  136.9 1.1 collective-permute-start
  137.9 8.9 %while.76 = (s32[]{:T(128)}, f32[1024]{0:T(1024)S(1)}, f32[3,512]{1,0:T(4,128)S(1)}, bf16[3,512,768]{2,1,0:T(8,128)(2,1)}, bf16[1024,768]{1,0:T(8,128)(2,1)}, /*index=5*/f32[3,512]{1,0:T(4,128)S(1)}, s32[]{:T(128)}, s32[]{:T(128)}) while((s32[]{:T(128)}, f32[1024]{0:T(1024)S(1)}, f32[3,512]{1,0:T(4,128)S(1)}, ...), condition=%wide.region_14.15_spmd.clone, body=%wide.region_11.14_spmd.clone.sunk | while | flops 807928320 | bytes 2388083 | solution.py:41
  137.9 2.9 %fusion.59 = (f32[512]{0:T(512)S(1)}, f32[1024]{0:T(1024)S(1)}) fusion(f32[512]{0:T(512)S(1)} %bitcast.101, bf16[1024,768]{1,0:T(8,128)(2,1)} %get-tuple-element.826, bf16[3,512,768]{2,1,0:T(8,128)(2,1)} %get-tuple-element.825, s32[]{:T(128)S(6)} %copy.23), kind=kOutput, calls=%fused_computation.14.clone.1 | convolution fusion | flops 807926272 | bytes 2367492 | tf_op jit(solution)/shard_map/while/body/eval_jaxpr/vd,rd->vr/dot_general | solution.py:37
  140.9 2.9 %fusion.59 = (f32[512]{0:T(512)S(1)}, f32[1024]{0:T(1024)S(1)}) fusion(f32[512]{0:T(512)S(1)} %bitcast.101, bf16[1024,768]{1,0:T(8,128)(2,1)} %get-tuple-element.826, bf16[3,512,768]{2,1,0:T(8,128)(2,1)} %get-tuple-element.825, s32[]{:T(128)S(6)} %copy.23), kind=kOutput, calls=%fused_computation.14.clone.1 | convolution fusion | flops 807926272 | bytes 2367492 | tf_op jit(solution)/shard_map/while/body/eval_jaxpr/vd,rd->vr/dot_general | solution.py:37
  143.9 2.9 %fusion.59 = (f32[512]{0:T(512)S(1)}, f32[1024]{0:T(1024)S(1)}) fusion(f32[512]{0:T(512)S(1)} %bitcast.101, bf16[1024,768]{1,0:T(8,128)(2,1)} %get-tuple-element.826, bf16[3,512,768]{2,1,0:T(8,128)(2,1)} %get-tuple-element.825, s32[]{:T(128)S(6)} %copy.23), kind=kOutput, calls=%fused_computation.14.clone.1 | convolution fusion | flops 807926272 | bytes 2367492 | tf_op jit(solution)/shard_map/while/body/eval_jaxpr/vd,rd->vr/dot_general | solution.py:37
  146.8 15.6 %collective-permute-done = f32[1024]{0:T(1024)S(1)} collective-permute-done((f32[1024]{0:T(1024)S(1)}, f32[1024]{0:T(1024)S(1)}, u32[]{:S(2)}, u32[]{:S(2)}) %collective-permute-start) | collective-permute-done | bytes 4128 | tf_op jit(solution)/shard_map/ppermute | solution.py:18
  162.5 5.0 %collective-permute-start.2 = (f32[1024]{0:T(1024)S(1)}, f32[1024]{0:T(1024)S(1)}, u32[]{:S(2)}, u32[]{:S(2)}) collective-permute-start(f32[1024]{0:T(1024)S(1)} %add.149), channel_id=1, source_target_pairs={{0,14},{2,0},{4,2},{6,4},{8,6},{10,8},{12,10},{14,12},{1,15},{3,1}... | collective-permute-start | bytes 12296 | tf_op jit(solution)/shard_map/ppermute | solution.py:18
  167.5 8.9 %while.77 = (s32[]{:T(128)}, f32[1024]{0:T(1024)S(1)}, f32[3,512]{1,0:T(4,128)S(1)}, bf16[3,512,768]{2,1,0:T(8,128)(2,1)}, bf16[1024,768]{1,0:T(8,128)(2,1)}, /*index=5*/f32[3,512]{1,0:T(4,128)S(1)}, s32[]{:T(128)}, s32[]{:T(128)}) while((s32[]{:T(128)}, f32[1024]{0:T(1024)S(1)}, f32[3,512]{1,0:T(4,128)S(1)}, ...), condition=%wide.region_18.19_spmd.clone, body=%wide.region_15.18_spmd.clone.sunk | while | flops 807928320 | bytes 2388083 | solution.py:41
  167.5 2.9 %fusion.61 = (f32[512]{0:T(512)S(1)}, f32[1024]{0:T(1024)S(1)}) fusion(f32[512]{0:T(512)S(1)} %bitcast.102, bf16[1024,768]{1,0:T(8,128)(2,1)} %get-tuple-element.850, bf16[3,512,768]{2,1,0:T(8,128)(2,1)} %get-tuple-element.849, s32[]{:T(128)S(6)} %copy.32), kind=kOutput, calls=%fused_computation.23.clone.1 | convolution fusion | flops 807926272 | bytes 2367492 | tf_op jit(solution)/shard_map/while/body/eval_jaxpr/vd,rd->vr/dot_general | solution.py:37
  170.4 2.9 %fusion.61 = (f32[512]{0:T(512)S(1)}, f32[1024]{0:T(1024)S(1)}) fusion(f32[512]{0:T(512)S(1)} %bitcast.102, bf16[1024,768]{1,0:T(8,128)(2,1)} %get-tuple-element.850, bf16[3,512,768]{2,1,0:T(8,128)(2,1)} %get-tuple-element.849, s32[]{:T(128)S(6)} %copy.32), kind=kOutput, calls=%fused_computation.23.clone.1 | convolution fusion | flops 807926272 | bytes 2367492 | tf_op jit(solution)/shard_map/while/body/eval_jaxpr/vd,rd->vr/dot_general | solution.py:37
  173.4 2.9 %fusion.61 = (f32[512]{0:T(512)S(1)}, f32[1024]{0:T(1024)S(1)}) fusion(f32[512]{0:T(512)S(1)} %bitcast.102, bf16[1024,768]{1,0:T(8,128)(2,1)} %get-tuple-element.850, bf16[3,512,768]{2,1,0:T(8,128)(2,1)} %get-tuple-element.849, s32[]{:T(128)S(6)} %copy.32), kind=kOutput, calls=%fused_computation.23.clone.1 | convolution fusion | flops 807926272 | bytes 2367492 | tf_op jit(solution)/shard_map/while/body/eval_jaxpr/vd,rd->vr/dot_general | solution.py:37
  176.8 8.9 %while.78 = (s32[]{:T(128)}, f32[1024]{0:T(1024)S(1)}, f32[3,512]{1,0:T(4,128)S(1)}, bf16[3,512,768]{2,1,0:T(8,128)(2,1)}, bf16[1024,768]{1,0:T(8,128)(2,1)}, /*index=5*/f32[3,512]{1,0:T(4,128)S(1)}, s32[]{:T(128)}, s32[]{:T(128)}) while((s32[]{:T(128)}, f32[1024]{0:T(1024)S(1)}, f32[3,512]{1,0:T(4,128)S(1)}, ...), condition=%wide.region_22.23_spmd.clone, body=%wide.region_19.22_spmd.clone.sunk | while | flops 807928320 | bytes 2388083 | solution.py:41
  176.9 2.9 %fusion.63 = (f32[512]{0:T(512)S(1)}, f32[1024]{0:T(1024)S(1)}) fusion(f32[512]{0:T(512)S(1)} %bitcast.103, bf16[1024,768]{1,0:T(8,128)(2,1)} %get-tuple-element.874, bf16[3,512,768]{2,1,0:T(8,128)(2,1)} %get-tuple-element.873, s32[]{:T(128)S(6)} %copy.41), kind=kOutput, calls=%fused_computation.32.clone.1 | convolution fusion | flops 807926272 | bytes 2367492 | tf_op jit(solution)/shard_map/while/body/eval_jaxpr/vd,rd->vr/dot_general | solution.py:37
  179.8 2.9 %fusion.63 = (f32[512]{0:T(512)S(1)}, f32[1024]{0:T(1024)S(1)}) fusion(f32[512]{0:T(512)S(1)} %bitcast.103, bf16[1024,768]{1,0:T(8,128)(2,1)} %get-tuple-element.874, bf16[3,512,768]{2,1,0:T(8,128)(2,1)} %get-tuple-element.873, s32[]{:T(128)S(6)} %copy.41), kind=kOutput, calls=%fused_computation.32.clone.1 | convolution fusion | flops 807926272 | bytes 2367492 | tf_op jit(solution)/shard_map/while/body/eval_jaxpr/vd,rd->vr/dot_general | solution.py:37
  182.8 2.9 %fusion.63 = (f32[512]{0:T(512)S(1)}, f32[1024]{0:T(1024)S(1)}) fusion(f32[512]{0:T(512)S(1)} %bitcast.103, bf16[1024,768]{1,0:T(8,128)(2,1)} %get-tuple-element.874, bf16[3,512,768]{2,1,0:T(8,128)(2,1)} %get-tuple-element.873, s32[]{:T(128)S(6)} %copy.41), kind=kOutput, calls=%fused_computation.32.clone.1 | convolution fusion | flops 807926272 | bytes 2367492 | tf_op jit(solution)/shard_map/while/body/eval_jaxpr/vd,rd->vr/dot_general | solution.py:37
  186.1 26.3 %collective-permute-done.7 = bf16[1024,768]{1,0:T(8,128)(2,1)S(1)} collective-permute-done((bf16[1024,768]{1,0:T(8,128)(2,1)}, bf16[1024,768]{1,0:T(8,128)(2,1)S(1)}, u32[]{:S(2)}, u32[]{:S(2)}) %collective-permute-start.7) | collective-permute-done | bytes 1572896 | tf_op jit(solution)/shard_map/ppermute | solution.py:18
  212.4 7.4 %while.79 = (s32[]{:T(128)}, f32[1024]{0:T(1024)S(1)}, f32[3,512]{1,0:T(4,128)S(1)}, bf16[3,512,768]{2,1,0:T(8,128)(2,1)}, bf16[1024,768]{1,0:T(8,128)(2,1)S(1)}...) while((s32[]{:T(128)}, f32[1024]{0:T(1024)S(1)}, f32[3,512]{1,0:T(4,128)S(1)}, ...), condition=%wide.region_26.27_spmd.clone, body=%wide.region_23.26_spmd.clone.sunk | while | flops 807928320 | bytes 2388083 | solution.py:41
  212.4 2.4 fusion.65
  214.9 2.4 fusion.65
  217.3 2.4 fusion.65
  219.9 2.5 %all-reduce = f32[1536]{0:T(1024)S(1)} all-reduce(f32[1536]{0:T(1024)S(1)} %add.157), channel_id=2, replica_groups=mesh['groups'=2,'blk'=8,'rep'=2] {'rep'}, use_global_device_ids=true, to_apply=%region_27.28.clone | all-reduce | flops 1536 | bytes 12288
  222.5 0.7 all_to_all.18
  223.1 6.0 %all-to-all-start.2 = ((f32[8,1,96]{2,1,0:T(1,128)}), f32[8,1,96]{2,1,0:T(1,128)S(1)}, u32[]{:S(2)}, u32[]{:S(2)}) async-start(f32[8,1,96]{2,1,0:T(1,128)} %all_to_all.18), calls=%async_computation.2 | async-start | bytes 8192 | tf_op jit(solution)/shard_map/all_to_all | solution.py:95
  229.7 5.9 %all-to-all-done.2 = f32[8,1,96]{2,1,0:T(1,128)S(1)} async-done(((f32[8,1,96]{2,1,0:T(1,128)}), f32[8,1,96]{2,1,0:T(1,128)S(1)}, u32[]{:S(2)}, u32[]{:S(2)}) %all-to-all-start.2) | async-done | bytes 3104 | tf_op jit(solution)/shard_map/all_to_all | solution.py:95
  236.9 2.3 gather_fusion
  (100 shorter events, 5.9 us)
Async XLA Ops:
  12.1 11.7 %copy-start = (bf16[1024,768]{1,0:T(8,128)(2,1)S(1)}, bf16[1024,768]{1,0:T(8,128)(2,1)}, u32[]{:S(2)}) copy-start(bf16[1024,768]{1,0:T(8,128)(2,1)} %param.13) | copy-start | bytes 4718596
  16.5 37.3 %all-to-all-start = ((bf16[8,96,768]{2,1,0:T(8,128)(2,1)}), bf16[8,96,768]{2,1,0:T(8,128)(2,1)S(1)}, u32[]{:S(2)}, u32[]{:S(2)}) async-start(bf16[8,96,768]{2,1,0:T(8,128)(2,1)} %bitcast.3), calls=%async_computation | async-start | bytes 2359296 | tf_op jit(solution)/shard_map/all_to_all | solution.py:65
  23.8 104.1 %all-gather.3.cloned.1.call-start = ((), (), s32[]{:S(2)}) async-start(), calls=%async_computation.3 | async-start | bytes 3538944 | tf_op jit(solution)/shard_map/all_gather | solution.py:77
  24.2 71.8 %copy-start.2 = (u32[32]{0:T(128)S(1)}, u32[32]{0:T(128)}, u32[]{:S(2)}) copy-start(u32[32]{0:T(128)} %constant.208) | copy-start | bytes 388
  25.8 51.4 %collective-permute-start.1 = (bf16[1024,768]{1,0:T(8,128)(2,1)}, bf16[1024,768]{1,0:T(8,128)(2,1)}, u32[]{:S(2)}, u32[]{:S(2)}) collective-permute-start(bf16[1024,768]{1,0:T(8,128)(2,1)} %fusion.26), channel_id=1, source_target_pairs={{0,14},{2,0},{4,2},{6,4},{8,6},{10,8},{12,10},{14,12},{1,15},{3,1}... | collective-permute-start | bytes 4718600 | tf_op jit(solution)/shard_map/ppermute | solution.py:18
  53.8 1.1 copy-start.1
  77.1 48.4 %collective-permute-start.3 = (bf16[1024,768]{1,0:T(8,128)(2,1)}, bf16[1024,768]{1,0:T(8,128)(2,1)}, u32[]{:S(2)}, u32[]{:S(2)}) collective-permute-start(bf16[1024,768]{1,0:T(8,128)(2,1)} %collective-permute-done.1), channel_id=1, source_target_pairs={{0,14},{2,0},{4,2},{6,4},{8,6},{10,8},{12,10},{14,12},{1,15},{3,1}... | collective-permute-start | bytes 4718600 | tf_op jit(solution)/shard_map/ppermute | solution.py:18
  91.0 32.6 %all-to-all-start.1 = ((bf16[8,1,96]{2,1,0:T(2,128)(2,1)}), bf16[8,1,96]{2,1,0:T(2,128)(2,1)S(1)}, u32[]{:S(2)}, u32[]{:S(2)}) async-start(bf16[8,1,96]{2,1,0:T(2,128)(2,1)} %all_to_all.20), calls=%async_computation.1 | async-start | bytes 8192 | tf_op jit(solution)/shard_map/all_to_all | solution.py:72
  125.6 50.9 %collective-permute-start.5 = (bf16[1024,768]{1,0:T(8,128)(2,1)}, bf16[1024,768]{1,0:T(8,128)(2,1)}, u32[]{:S(2)}, u32[]{:S(2)}) collective-permute-start(bf16[1024,768]{1,0:T(8,128)(2,1)} %collective-permute-done.3), channel_id=1, source_target_pairs={{0,14},{2,0},{4,2},{6,4},{8,6},{10,8},{12,10},{14,12},{1,15},{3,1}... | collective-permute-start | bytes 4718600 | tf_op jit(solution)/shard_map/ppermute | solution.py:18
  136.9 25.6 %collective-permute-start = (f32[1024]{0:T(1024)S(1)}, f32[1024]{0:T(1024)S(1)}, u32[]{:S(2)}, u32[]{:S(2)}) collective-permute-start(f32[1024]{0:T(1024)S(1)} %get-tuple-element.392), channel_id=1, source_target_pairs={{0,14},{2,0},{4,2},{6,4},{8,6},{10,8},{12,10},{14,12},{1,15},{3,1}... | collective-permute-start | bytes 12296 | tf_op jit(solution)/shard_map/ppermute | solution.py:18
  162.5 13.9 %collective-permute-start.2 = (f32[1024]{0:T(1024)S(1)}, f32[1024]{0:T(1024)S(1)}, u32[]{:S(2)}, u32[]{:S(2)}) collective-permute-start(f32[1024]{0:T(1024)S(1)} %add.149), channel_id=1, source_target_pairs={{0,14},{2,0},{4,2},{6,4},{8,6},{10,8},{12,10},{14,12},{1,15},{3,1}... | collective-permute-start | bytes 12296 | tf_op jit(solution)/shard_map/ppermute | solution.py:18
  176.4 9.4 %collective-permute-start.4 = (f32[1024]{0:T(1024)S(1)}, f32[1024]{0:T(1024)S(1)}, u32[]{:S(2)}, u32[]{:S(2)}) collective-permute-start(f32[1024]{0:T(1024)S(1)} %add.150), channel_id=1, source_target_pairs={{0,14},{2,0},{4,2},{6,4},{8,6},{10,8},{12,10},{14,12},{1,15},{3,1}... | collective-permute-start | bytes 12296 | tf_op jit(solution)/shard_map/ppermute | solution.py:18
  176.5 35.9 %collective-permute-start.7 = (bf16[1024,768]{1,0:T(8,128)(2,1)}, bf16[1024,768]{1,0:T(8,128)(2,1)S(1)}, u32[]{:S(2)}, u32[]{:S(2)}) collective-permute-start(bf16[1024,768]{1,0:T(8,128)(2,1)} %collective-permute-done.5), channel_id=1, source_target_pairs={{0,14},{2,0},{4,2},{6,4},{8,6},{10,8},{12,10},{14,12},{1,15},{3,1}... | collective-permute-start | bytes 4718600 | tf_op jit(solution)/shard_map/ppermute | solution.py:18
  185.8 34.0 %collective-permute-start.6 = (f32[1024]{0:T(1024)S(1)}, f32[1024]{0:T(1024)S(1)}, u32[]{:S(2)}, u32[]{:S(2)}) collective-permute-start(f32[1024]{0:T(1024)S(1)} %add.151), channel_id=1, source_target_pairs={{0,14},{2,0},{4,2},{6,4},{8,6},{10,8},{12,10},{14,12},{1,15},{3,1}... | collective-permute-start | bytes 12296 | tf_op jit(solution)/shard_map/ppermute | solution.py:18
  219.8 9.3 %collective-permute-start.8 = (f32[1024]{0:T(1024)S(1)}, f32[1024]{0:T(1024)S(1)}, u32[]{:S(2)}, u32[]{:S(2)}) collective-permute-start(f32[1024]{0:T(1024)S(1)} %add.152), channel_id=1, source_target_pairs={{0,8},{2,10},{4,12},{6,14},{8,0},{10,2},{12,4},{14,6},{1,9},{3,11}... | collective-permute-start | bytes 12296 | tf_op jit(solution)/shard_map/ppermute | solution.py:18
  223.1 12.4 %all-to-all-start.2 = ((f32[8,1,96]{2,1,0:T(1,128)}), f32[8,1,96]{2,1,0:T(1,128)S(1)}, u32[]{:S(2)}, u32[]{:S(2)}) async-start(f32[8,1,96]{2,1,0:T(1,128)} %all_to_all.18), calls=%async_computation.2 | async-start | bytes 8192 | tf_op jit(solution)/shard_map/all_to_all | solution.py:95
Sparse Core Ops, SparseCore 0:
  55.0 41.4 all-gather.2
where the time goes:
time: 248 us; the launch traced here: 247 us
  waiting for transfers between devices  120 us (48%)
  matrix products  41.6 us (17%)
  starting transfers between devices  41.5 us (17%)
  between operations  14.8 us (6%)
  local copies, waits for them, and re-layouts  12.1 us (5%)
  other arithmetic  11.8 us (5%)
  blocking collectives  4.32 us (2%)
    ppermute x9, waiting for transfers between devices, shifted(): return lax.ppermute(value, axis, pairs)  64.2 us
    dot_general x15, matrix products, tile_sums(): jnp.einsum('vd,rd->vr', visit_tile, residents, preferred_element_type=jnp...  41.6 us
    all_to_all x1, waiting for transfers between devices, on_device(): lax.all_to_all(filled.reshape(cycle_size, slot_count), 'blk', split_axis=...  26.5 us
    all_to_all x1, waiting for transfers between devices, on_device(): lax.all_to_all(outgoing.reshape(cycle_size, slot_count, columns), 'blk',...  23.3 us
    ppermute x9, starting transfers between devices, shifted(): return lax.ppermute(value, axis, pairs)  23.3 us
    all_to_all x1, starting transfers between devices, on_device(): lax.all_to_all(outgoing.reshape(cycle_size, slot_count, columns), 'blk',...  7.31 us
    all_to_all x1, starting transfers between devices, on_device(): lax.all_to_all(own_sums.reshape(cycle_size, slot_count), 'blk', split_axi...  5.96 us
    all_to_all x1, waiting for transfers between devices, on_device(): lax.all_to_all(own_sums.reshape(cycle_size, slot_count), 'blk', split_axi...  5.87 us
  transfers between devices with their start and end apart: 13, of which 6 were waited for; matrix products, arithmetic and copies ran while one was open for 20% of the time, Pallas kernels for 0%

commit v1 on v0

v1 whole, which is shorter than its diff:
```python
import functools

import jax
import jax.numpy as jnp
from jax import lax
from jax.experimental import pallas as pl
from jax.experimental.pallas import tpu as pltpu
from jax.sharding import PartitionSpec as P


CL_OWN = 16
CYCLE_STEPS = 4
INGEST_DEV = 512

temper = 0.2
epsilon = 1e-06


GAIN = 1.4426950408889634 / temper
OFF = -1e30
LANES = 128
NT = (((1,), (1,)), ((), ()))
VMEM = pl.BlockSpec(memory_space=pltpu.VMEM)
TILE = 512
FIRST = 8


def unit_body(parts, n_more, x_ref, *refs):
    for part, o_ref in zip(parts, refs[n_more:]):
        values = x_ref[part, :].astype(jnp.float32)
        squares = jnp.sum(values * values, axis=-1, keepdims=True) + epsilon
        o_ref[...] = (values * lax.rsqrt(squares)).astype(jnp.bfloat16)


def unit_rows_call(rows, parts, more):
    columns = rows.shape[1]
    sizes = [part.stop - part.start for part in parts]
    return pl.pallas_call(
        functools.partial(unit_body, parts, len(more)),
        in_specs=[VMEM] * (1 + len(more)),
        out_specs=[VMEM] * len(parts),
        out_shape=[pltpu.VMEM((size, columns), jnp.bfloat16) for size in sizes],
        compiler_params=pltpu.CompilerParams(vmem_limit_bytes=24 * 2**20),
        cost_estimate=pl.CostEstimate(
            flops=sum(sizes) * columns * 300, bytes_accessed=sum(sizes) * columns * 4, transcendentals=sum(sizes)
        ),
    )(rows, *more)


def sums_body(n_docs, n_res, cycle, cuts, sides, doc_in, res_in, *refs):
    refs = list(refs)
    place_ref = refs.pop(0)
    docs = [refs.pop(0) for _ in range(n_docs)]
    owners = [refs.pop(0) for _ in range(n_docs)]
    res = [refs.pop(0) for _ in range(n_res)]
    doc_prev = [refs.pop(0) if f else None for f in doc_in]
    res_prev = [refs.pop(0) if f else None for f in res_in]
    doc_out = [refs.pop(0) for _ in range(n_docs)]
    res_out = [refs.pop(0) for _ in range(n_res)]
    work = []
    for i in range(n_docs):
        for j in range(n_res):
            rows = res[j].shape[0]
            tile = min(TILE, rows)
            work += [(i, j, t, tile) for t in range(0, rows, tile)]

    def scores(i, j, t, tile):
        return lax.dot_general(
            docs[i][...], res[j][t : t + tile, :], NT, preferred_element_type=jnp.float32
        )

    seen = set()
    doing = None
    ahead = scores(*work[0])
    for w, (i, j, t, tile) in enumerate(work):
        n = docs[i].shape[0]
        if doing != i:
            doing = i
            bias = {}
            for side in sorted(set(sides)):
                steps = place_ref[side : side + 1, :n] - owners[i][:, cuts[i]]
                steps = jnp.where(steps < 0, steps + cycle, steps)
                row = jnp.where(steps <= CYCLE_STEPS, -GAIN, OFF).astype(jnp.float32)
                bias[side] = jnp.broadcast_to(row, (LANES, n)).T
            total = jnp.zeros((n, LANES), jnp.float32)
        s = ahead
        if w + 1 < len(work):
            ahead = scores(*work[w + 1])
        for q in range(0, tile, LANES):
            k = jnp.exp2(s[:, q : q + LANES] * GAIN + bias[sides[j]])
            total = total + k
            part = jnp.sum(k, axis=0, keepdims=True)
            col = slice(t + q, t + q + LANES)
            if (j, t + q) in seen:
                part = part + res_out[j][:, col]
            elif res_prev[j] is not None:
                part = part + res_prev[j][:, col]
            seen.add((j, t + q))
            res_out[j][:, col] = part
        if w + 1 == len(work) or work[w + 1][0] != i:
            row = jnp.sum(total.T, axis=0, keepdims=True)
            if doc_prev[i] is not None:
                row = row + doc_prev[i][...]
            doc_out[i][...] = row


def held(value):
    return pltpu.with_memory_space_constraint(value, pltpu.VMEM)


def kernel_sums(cycle, place, chunks, res, sides, doc_prev, res_prev):
    docs, owners, cuts = zip(*chunks)
    doc_in = tuple(x is not None for x in doc_prev)
    res_in = tuple(x is not None for x in res_prev)
    n = sum(x.shape[0] for x in docs)
    m = sum(x.shape[0] for x in res)
    docs = [held(x) for x in docs]
    res = [held(x) for x in res]
    operands = [place, *docs, *owners, *res]
    operands += [x for x in doc_prev if x is not None]
    operands += [x for x in res_prev if x is not None]
    out = pl.pallas_call(
        functools.partial(sums_body, len(docs), len(res), cycle, cuts, tuple(sides), doc_in, res_in),
        in_specs=[VMEM] * len(operands),
        out_specs=[VMEM] * (len(docs) + len(res)),
        out_shape=[jax.ShapeDtypeStruct((1, x.shape[0]), jnp.float32) for x in (*docs, *res)],
        compiler_params=pltpu.CompilerParams(vmem_limit_bytes=24 * 2**20),
        cost_estimate=pl.CostEstimate(
            flops=2 * n * m * docs[0].shape[1], bytes_accessed=(n + m) * 1536, transcendentals=n * m
        ),
    )(*operands)
    return list(out[: len(docs)]), list(out[len(docs) :])


def line_order(count):
    return list(range(0, count, 2)) + list(reversed(range(1, count, 2)))


def dense(resident, ingest, cluster_ids):
    return dense_body(resident, ingest, cluster_ids)


def dense_body(resident, ingest, cluster_ids):
    cycle = lax.axis_size("blk")
    lines = cycle // 2
    order = line_order(lines)
    count, _ = ingest.shape
    cuts = (0, count * FIRST // 16, count)
    parts = [slice(cuts[k], cuts[k + 1]) for k in range(2)]

    def along(value, steps):
        pairs = [
            (order[k] * 2 + y, order[(k + steps) % lines] * 2 + y) for k in range(lines) for y in range(2)
        ]
        return lax.ppermute(value, "blk", pairs)

    def mate(value):
        return lax.ppermute(value, "blk", [(p, p ^ 1) for p in range(cycle)])

    def twin(value):
        return lax.ppermute(value, "rep", [(0, 1), (1, 0)])

    here = lax.axis_index("blk")
    place = jnp.stack([here, here ^ 1]).astype(jnp.int32)
    place = jnp.broadcast_to(place[:, None], (2, count))

    own = [unit_rows_call(ingest, [parts[k]], [resident])[0] for k in range(2)]
    units = [own]
    owners = [(cluster_ids // CL_OWN).reshape(1, count)]
    for d in range(1, lines):
        units.append([along(units[-1][k], 1) for k in range(2)])
        owners.append(along(owners[-1], 1))
    chunks = [[(units[d][k], owners[d], parts[k]) for k in range(2)] for d in range(lines)]

    rows = resident.shape[0]
    whole = slice(0, rows)
    halves = [slice(0, rows // 2), slice(rows // 2, rows)]
    r0, *r0_halves = unit_rows_call(resident, [whole, *halves], [])
    r2 = [mate(r0_halves[k]) for k in range(2)]
    r1 = twin(r0)
    r3 = [twin(r2[k]) for k in range(2)]
    ra = [r2[0], r3[0]]
    rb = [r2[1], r3[1]]

    def sums(docs, res, sides, doc_prev, res_prev):
        return kernel_sums(cycle, place, docs, res, sides, doc_prev, res_prev)

    d_own, a0 = sums(chunks[0], [r0], [0], [None] * 2, [None])
    d_own, a1 = sums(chunks[0], [r1], [0], d_own, [None])
    a = a0 + a1
    d1, d2 = [], []
    for k in range(2):
        d, a = sums(chunks[1][k : k + 1], [r0, r1], [0, 0], [None], a)
        d1 += d
    d, aa = sums(chunks[0] + chunks[1], ra, [1, 1], d_own + d1, [None] * 2)
    d_own, d1 = d[:2], d[2:]
    a = a + aa
    for k in range(2):
        d, a = sums(chunks[2][k : k + 1], [r0, r1, *ra], [0, 0, 1, 1], [None], a)
        d2 += d
    d, ab = sums(chunks[0] + chunks[1] + chunks[2], rb, [1, 1], d_own + d1 + d2, [None] * 2)
    d_own, d1, d2 = d[:2], d[2:4], d[4:]
    d3a, a = sums(chunks[3][:1], [r0, r1, *ra, *rb], [0, 0, 1, 1, 1, 1], [None], a + ab)
    d3b, am = sums(chunks[3][1:], ra + rb, [1] * 4, [None], a[2:])
    to_mate = jnp.concatenate([am[0], am[2], am[1], am[3]], axis=1)
    from_mate = mate(to_mate)
    d3b, an = sums(chunks[3][1:], [r0, r1], [0, 0], d3b, a[:2])
    to_twin = an[1] + from_mate[:, rows:]
    from_twin = twin(to_twin)
    resident_density = an[0] + from_mate[:, :rows] + from_twin

    ingest_density = jnp.concatenate(d_own, axis=1)
    for d, pieces in ((1, d1), (2, d2), (3, d3a + d3b)):
        pieces = jnp.concatenate(pieces, axis=1)
        ingest_density = ingest_density + along(pieces, -d)
    return (jnp.log1p(resident_density).reshape(-1), jnp.log1p(ingest_density).reshape(-1))


def shifted(value, axis, steps):
    count = lax.axis_size(axis)
    pairs = [(source, (source + steps) % count) for source in range(count)]
    return lax.ppermute(value, axis, pairs)


def unit_rows(rows):
    values = rows.astype(jnp.float32)
    squares = jnp.sum(values * values, axis=-1, keepdims=True) + epsilon
    factor = lax.rsqrt(squares)
    return (values * factor).astype(jnp.bfloat16)


def scanned_sums(visitors, occupancy, residents):
    count_rows = visitors.shape[0]
    block_rows = 512
    num_blocks = count_rows // block_rows
    visit_blocks = visitors.reshape(num_blocks, block_rows, visitors.shape[1])
    live_blocks = occupancy.astype(jnp.float32).reshape(num_blocks, block_rows)

    def tile_sums(running, pieces):
        visit_tile, live_tile = pieces
        scores = jnp.einsum("vd,rd->vr", visit_tile, residents, preferred_element_type=jnp.float32)
        kernel = jnp.exp((scores - 1.0) / temper)
        return (running + jnp.sum(kernel * live_tile[:, None], axis=0), jnp.sum(kernel, axis=1))

    resident_part, visit_parts = lax.scan(
        tile_sums, jnp.zeros((residents.shape[0],), jnp.float32), (visit_blocks, live_blocks)
    )
    return (visit_parts.reshape(count_rows), resident_part)


def cyclic(resident, ingest, cluster_ids):
    cycle_size = lax.axis_size("blk")
    slot_count = 3 * INGEST_DEV // (2 * cycle_size)
    columns = ingest.shape[1]
    owners = cluster_ids // CL_OWN
    onehot = (owners[:, None] == jnp.arange(cycle_size, dtype=jnp.int32)[None, :]).astype(jnp.int32)
    rank_within = jnp.sum((jnp.cumsum(onehot, axis=0) - onehot) * onehot, axis=1)
    targets = owners * slot_count + rank_within
    unit_ingest = unit_rows(ingest)
    outgoing = jnp.zeros((cycle_size * slot_count, columns), jnp.bfloat16).at[targets].set(unit_ingest)
    filled = (
        jnp.zeros((cycle_size * slot_count,), jnp.bfloat16)
        .at[targets]
        .set(jnp.ones((ingest.shape[0],), jnp.bfloat16))
    )
    exchange = functools.partial(lax.all_to_all, axis_name="blk", split_axis=0, concat_axis=0, tiled=True)
    arrived = exchange(outgoing.reshape(cycle_size, slot_count, columns))
    present = exchange(filled.reshape(cycle_size, slot_count))
    visitors = lax.all_gather(arrived.reshape(cycle_size * slot_count, columns), "rep", axis=0, tiled=True)
    marked = lax.all_gather(present.reshape(cycle_size * slot_count), "rep", axis=0, tiled=True)
    visit_total = jnp.zeros((visitors.shape[0],), jnp.float32)
    resident_total = jnp.zeros((resident.shape[0],), jnp.float32)
    moving = unit_rows(resident)
    for rotation in range(CYCLE_STEPS + 1):
        if rotation > 0:
            moving = shifted(moving, "blk", -1)
            resident_total = shifted(resident_total, "blk", -1)
        visit_part, resident_part = scanned_sums(visitors, marked, moving)
        visit_total = visit_total + visit_part
        resident_total = resident_total + resident_part
    resident_total = shifted(resident_total, "blk", CYCLE_STEPS)
    own_sums = lax.psum_scatter(visit_total, "rep", scatter_dimension=0, tiled=True)
    returned = exchange(own_sums.reshape(cycle_size, slot_count))
    density = returned.reshape(cycle_size * slot_count)[targets]
    return (jnp.log1p(resident_total), jnp.log1p(density))


def solution(mesh):
    spread = ("groups", "blk", "rep")
    in_specs = (P(spread, None), P(spread, None), P(spread))
    out_specs = (P(spread), P(spread))
    short = mesh.shape["blk"] == 8 and mesh.shape["rep"] == 2
    return jax.shard_map(
        dense if short else cyclic, mesh=mesh, in_specs=in_specs, out_specs=out_specs, check_vma=False
    )
```

time: 248 us -> 88.6 us (0.36)
  waiting for transfers between devices: 120 us -> 20.7 us
  matrix products: 41.6 us -> 0 us
  Pallas kernels: 0 us -> 30 us
  between operations: 14.8 us -> 0.77 us
  starting transfers between devices: 41.5 us -> 29.9 us
  other arithmetic: 11.8 us -> 1.33 us
  local copies, waits for them, and re-layouts: 12.1 us -> 5.38 us
  blocking collectives: 4.32 us -> 0 us
    all_to_all x3 -> x0, waiting for transfers between devices: 55.7 us -> none  [the longest x1 26.5 us: on_device(): lax.all_to_all(filled.reshape(cycle_size, slot_count), 'blk', split_axis=...]
    ppermute x9 -> x19, waiting for transfers between devices: 64.2 us -> 20.7 us  [the longest x12 16.3 us: along(): return lax.ppermute(value, 'blk', pairs)]
    dot_general x15 -> x0, matrix products: 41.6 us -> none  [tile_sums(): jnp.einsum('vd,rd->vr', visit_tile, residents, preferred_element_type=jnp...]
    pallas_call x0 -> x14, Pallas kernels: none -> 30 us  [the longest x11 27.8 us: kernel_sums(): pl.pallas_call(functools.partial(sums_body, len(docs), len(res), cycle, c...]
    all_to_all x3 -> x0, starting transfers between devices: 18.2 us -> none  [the longest x1 7.31 us: on_device(): lax.all_to_all(outgoing.reshape(cycle_size, slot_count, columns), 'blk',...]
    ppermute x9 -> x19, starting transfers between devices: 23.3 us -> 29.9 us  [the longest x12 25.3 us: along(): return lax.ppermute(value, 'blk', pairs)]
    scatter x1 -> x0, other arithmetic: 4.35 us -> none  [on_device(): jnp.zeros((cycle_size * slot_count, columns), jnp.bfloat16).at[targets]]
    scatter x1 -> x0, local copies, waits for them, and re-layouts: 3.77 us -> none  [on_device(): filled = jnp.zeros((cycle_size * slot_count,), jnp.bfloat16).at[targets]....]
  transfers between devices with their start and end apart: 13 -> 19, of which waited for: 6 -> 5; matrix products, arithmetic and copies ran while one was open for 20% -> 1% of each run, Pallas kernels for 0% -> 32%
where the time goes in v1:
time: 88.6 us; the launch traced here: 88 us
  Pallas kernels  30 us (34%)
  starting transfers between devices  29.9 us (34%)
  waiting for transfers between devices  20.7 us (23%)
  local copies, waits for them, and re-layouts  5.38 us (6%)
  other arithmetic  1.33 us (2%)
    pallas_call x11, Pallas kernels, kernel_sums(): pl.pallas_call(functools.partial(sums_body, len(docs), len(res), cycle, c...  27.8 us
    ppermute x12, starting transfers between devices, along(): return lax.ppermute(value, 'blk', pairs)  25.3 us
    ppermute x12, waiting for transfers between devices, along(): return lax.ppermute(value, 'blk', pairs)  16.3 us
    unnamed x16, local copies, waits for them, and re-layouts  5.3 us
    ppermute x3, waiting for transfers between devices, mate(): return lax.ppermute(value, 'blk', [(p, p ^ 1) for p in range(cycle)])  4.37 us
    ppermute x3, starting transfers between devices, mate(): return lax.ppermute(value, 'blk', [(p, p ^ 1) for p in range(cycle)])  3.97 us
    pallas_call x3, Pallas kernels, unit_rows_call(): pl.pallas_call(functools.partial(unit_body, parts, len(more)), in_specs=[...  2.19 us
  transfers between devices with their start and end apart: 19, of which 5 were waited for; matrix products, arithmetic and copies ran while one was open for 1% of the time, Pallas kernels for 32%

profile of v1, /device:TPU:0, one launch (start us, length us, event | category | flops | bytes accessed | tf_op | source)
XLA Modules:
  0.0 88.0 jit_solution(4208590432936829260)
XLA Ops:
  0.6 1.4 %copy-done = bf16[1024,768]{1,0:T(8,128)(2,1)S(1)} copy-done((bf16[1024,768]{1,0:T(8,128)(2,1)S(1)}, bf16[1024,768]{1,0:T(8,128)(2,1)}, u32[]{:S(2)}) %copy-start) | copy-done | bytes 1572888
  2.0 1.9 %shard_map.51 = (bf16[1024,768]{1,0:T(8,128)(2,1)S(1)}, bf16[512,768]{1,0:T(8,128)(2,1)S(1)}, bf16[512,768]{1,0:T(8,128)(2,1)}) custom-call(bf16[1024,768]{1,0:T(8,128)(2,1)S(1)} %copy-done), custom_call_target="tpu_custom_call" | custom-call | flops 471859200 | bytes 6291456 | tf_op jit(solution)/shard_map/pallas_call | solution.py:38
  3.9 0.5 collective-permute-start.6
  4.4 2.5 %collective-permute-start.7 = (bf16[512,768]{1,0:T(8,128)(2,1)S(1)}, bf16[512,768]{1,0:T(8,128)(2,1)}, u32[]{:S(2)}, u32[]{:S(2)}) collective-permute-start(bf16[512,768]{1,0:T(8,128)(2,1)S(1)} %get-tuple-element.57), channel_id=1, source_target_pairs={{0,2},{2,0},{4,6},{6,4},{8,10},{10,8},{12,14},{14,12},{1,3},{3,1},... | collective-permute-start | bytes 2359304 | tf_op jit(solution)/shard_map/ppermute | solution.py:158
  6.9 0.0 collective-permute-start.9
  6.9 3.1 %collective-permute-start.3 = (s32[1,512]{1,0:T(1,128)S(1)}, s32[1,512]{1,0:T(1,128)S(1)}, u32[]{:S(2)}, u32[]{:S(2)}) collective-permute-start(s32[1,512]{1,0:T(1,128)S(1)} %bitcast.5), channel_id=1, source_target_pairs={{0,8},{2,10},{8,12},{10,14},{12,4},{14,6},{4,0},{6,2},{1,9},{3,11}... | collective-permute-start | bytes 6152 | tf_op jit(solution)/shard_map/ppermute | solution.py:155
  10.1 1.1 %copy-done.2 = bf16[512,768]{1,0:T(8,128)(2,1)S(1)} copy-done((bf16[512,768]{1,0:T(8,128)(2,1)S(1)}, bf16[512,768]{1,0:T(8,128)(2,1)}, u32[]{:S(2)}) %copy-start.2) | copy-done | bytes 786456
  11.2 0.2 shard_map.52.refs_1_
  11.4 1.6 %collective-permute-start.11 = (bf16[256,768]{1,0:T(8,128)(2,1)S(1)}, bf16[256,768]{1,0:T(8,128)(2,1)}, u32[]{:S(2)}, u32[]{:S(2)}) collective-permute-start(bf16[256,768]{1,0:T(8,128)(2,1)S(1)} %shard_map.52.refs_1_), channel_id=1, source_target_pairs={{0,8},{2,10},{8,12},{10,14},{12,4},{14,6},{4,0},{6,2},{1,9},{3,11}... | collective-permute-start | bytes 1179656 | tf_op jit(solution)/shard_map/ppermute | solution.py:155
  13.0 1.5 %collective-permute-start.4 = (s32[1,512]{1,0:T(1,128)S(1)}, s32[1,512]{1,0:T(1,128)S(1)}, u32[]{:S(2)}, u32[]{:S(2)}) collective-permute-start(s32[1,512]{1,0:T(1,128)S(1)} %collective-permute-done.3.refs_2_.refs_7_.refs_8_.refs_9_.refs_10_), channel_id=1, source_target_pairs={{0,8},{2,10},{8,12},{10,14},{12,4},{14,6},{4,0},{6,2},{1,9},{3,11}... | collective-permute-start | bytes 6152 | tf_op jit(solution)/shard_map/ppermute | solution.py:155
  14.6 0.2 shard_map.50.refs_2_
  14.7 7.5 %collective-permute-done.4.refs_2_.refs_11_.refs_12_ = s32[1,512]{1,0:T(1,128)S(1)} collective-permute-done((s32[1,512]{1,0:T(1,128)S(1)}, s32[1,512]{1,0:T(1,128)S(1)}, u32[]{:S(2)}, u32[]{:S(2)}) %collective-permute-start.4) | collective-permute-done | bytes 2080 | tf_op jit(solution)/shard_map/ppermute | solution.py:155
  22.2 2.5 %collective-permute-start = (bf16[256,768]{1,0:T(8,128)(2,1)S(1)}, bf16[256,768]{1,0:T(8,128)(2,1)}, u32[]{:S(2)}, u32[]{:S(2)}) collective-permute-start(bf16[256,768]{1,0:T(8,128)(2,1)S(1)} %shard_map.50.refs_2_), channel_id=1, source_target_pairs={{0,8},{2,10},{8,12},{10,14},{12,4},{14,6},{4,0},{6,2},{1,9},{3,11}... | collective-permute-start | bytes 1179656 | tf_op jit(solution)/shard_map/ppermute | solution.py:155
  24.7 0.8 copy-done.5
  25.5 0.0 collective-permute-done.7.refs_9_.refs_5_.refs_3_
  25.5 3.0 %collective-permute-start.12 = (bf16[256,768]{1,0:T(8,128)(2,1)}, bf16[256,768]{1,0:T(8,128)(2,1)}, u32[]{:S(2)}, u32[]{:S(2)}) collective-permute-start(bf16[256,768]{1,0:T(8,128)(2,1)} %collective-permute-done.11.refs_1_.refs_3_), channel_id=1, source_target_pairs={{0,8},{2,10},{8,12},{10,14},{12,4},{14,6},{4,0},{6,2},{1,9},{3,11}... | collective-permute-start | bytes 1179656 | tf_op jit(solution)/shard_map/ppermute | solution.py:155
  28.5 5.8 %collective-permute-done.refs_1_.refs_4_ = bf16[256,768]{1,0:T(8,128)(2,1)} collective-permute-done((bf16[256,768]{1,0:T(8,128)(2,1)S(1)}, bf16[256,768]{1,0:T(8,128)(2,1)}, u32[]{:S(2)}, u32[]{:S(2)}) %collective-permute-start) | collective-permute-done | bytes 393248 | tf_op jit(solution)/shard_map/ppermute | solution.py:155
  34.3 3.4 %collective-permute-start.1 = (bf16[256,768]{1,0:T(8,128)(2,1)}, bf16[256,768]{1,0:T(8,128)(2,1)S(1)}, u32[]{:S(2)}, u32[]{:S(2)}) collective-permute-start(bf16[256,768]{1,0:T(8,128)(2,1)} %collective-permute-done.refs_1_.refs_4_), channel_id=1, source_target_pairs={{0,8},{2,10},{8,12},{10,14},{12,4},{14,6},{4,0},{6,2},{1,9},{3,11}... | collective-permute-start | bytes 1179656 | tf_op jit(solution)/shard_map/ppermute | solution.py:155
  37.7 4.4 %collective-permute-done.9.refs_13_.refs_7_.refs_5_ = bf16[512,768]{1,0:T(8,128)(2,1)} collective-permute-done((bf16[512,768]{1,0:T(8,128)(2,1)}, bf16[512,768]{1,0:T(8,128)(2,1)}, u32[]{:S(2)}, u32[]{:S(2)}) %collective-permute-start.9) | collective-permute-done | bytes 786464 | tf_op jit(solution)/shard_map/ppermute | solution.py:158
  42.1 0.0 collective-permute-start.10
  42.1 0.1 pad_add_fusion
  42.2 0.1 broadcast_in_dim.2.refs_0_
  42.2 1.0 %copy-done.4 = bf16[256,768]{1,0:T(8,128)(2,1)S(1)} copy-done((bf16[256,768]{1,0:T(8,128)(2,1)S(1)}, bf16[256,768]{1,0:T(8,128)(2,1)}, u32[]{:S(2)}) %copy-start.4) | copy-done | bytes 393240
  43.2 1.0 %copy-done.6 = bf16[256,768]{1,0:T(8,128)(2,1)S(1)} copy-done((bf16[256,768]{1,0:T(8,128)(2,1)S(1)}, bf16[256,768]{1,0:T(8,128)(2,1)}, u32[]{:S(2)}) %copy-start.6) | copy-done | bytes 393240
  44.2 1.1 %shard_map.53 = (f32[1,256]{1,0:T(1,128)S(1)}, f32[1,256]{1,0:T(1,128)S(1)}, f32[1,1024]{1,0:T(1,128)S(1)}) custom-call(s32[2,512]{1,0:T(2,128)S(1)} %broadcast_in_dim.2.refs_0_, bf16[256,768]{1,0:T(8,128)(2,1)S(1)} %copy-done.4, bf16[256,768]{1,0:T(8,128)(2,1)S(1)} %copy-done.6, s32[1,512]{1,0:T(1,128)S(1)} %bitcast.6, s32[1,512]{1,0:T(1,128)S(1)} %bitcast.7, ...), custom_call_target="tpu_custom_call" | custom-call | flops 805306368 | bytes 2359296 | tf_op jit(solution)/shard_map/pallas_call | solution.py:122
  45.3 0.0 collective-permute-done.12.refs_1_.refs_5_
  45.4 2.9 %collective-permute-start.5 = (s32[1,512]{1,0:T(1,128)S(1)}, s32[1,512]{1,0:T(1,128)S(1)}, u32[]{:S(2)}, u32[]{:S(2)}) collective-permute-start(s32[1,512]{1,0:T(1,128)S(1)} %collective-permute-done.4.refs_2_.refs_11_.refs_12_), channel_id=1, source_target_pairs={{0,8},{2,10},{8,12},{10,14},{12,4},{14,6},{4,0},{6,2},{1,9},{3,11}... | collective-permute-start | bytes 6152 | tf_op jit(solution)/shard_map/ppermute | solution.py:155
  48.2 0.9 collective-permute-done.1.refs_1_.refs_6_
  49.1 3.3 %collective-permute-start.13 = (bf16[256,768]{1,0:T(8,128)(2,1)}, bf16[256,768]{1,0:T(8,128)(2,1)S(1)}, u32[]{:S(2)}, u32[]{:S(2)}) collective-permute-start(bf16[256,768]{1,0:T(8,128)(2,1)} %collective-permute-done.12.refs_1_.refs_5_), channel_id=1, source_target_pairs={{0,8},{2,10},{8,12},{10,14},{12,4},{14,6},{4,0},{6,2},{1,9},{3,11}... | collective-permute-start | bytes 1179656 | tf_op jit(solution)/shard_map/ppermute | solution.py:155
  52.4 0.0 collective-permute-start.2
  52.4 1.1 %shard_map.54 = (f32[1,256]{1,0:T(1,128)S(1)}, f32[1,256]{1,0:T(1,128)S(1)}, f32[1,1024]{1,0:T(1,128)S(1)}) custom-call(s32[2,512]{1,0:T(2,128)S(1)} %broadcast_in_dim.2.refs_0_, bf16[256,768]{1,0:T(8,128)(2,1)S(1)} %copy-done.4, bf16[256,768]{1,0:T(8,128)(2,1)S(1)} %copy-done.6, s32[1,512]{1,0:T(1,128)S(1)} %bitcast.8, s32[1,512]{1,0:T(1,128)S(1)} %bitcast.9, ...), custom_call_target="tpu_custom_call" | custom-call | flops 805306368 | bytes 2359296 | tf_op jit(solution)/shard_map/pallas_call | solution.py:122
  53.5 2.1 %shard_map.55 = (f32[1,256]{1,0:T(1,128)S(1)}, f32[1,1024]{1,0:T(1,128)S(1)}, f32[1,1024]{1,0:T(1,128)S(1)}) custom-call(s32[2,512]{1,0:T(2,128)S(1)} %broadcast_in_dim.2.refs_0_, bf16[256,768]{1,0:T(8,128)(2,1)} %collective-permute-done.11.refs_1_.refs_3_, s32[1,512]{1,0:T(1,128)S(1)} %collective-permute-done.3.refs_2_.refs_7_.refs_8_.refs_9_.refs_10_, ...), custom_call_target="tpu_custom_call" | custom-call | flops 805306368 | bytes 3538944 | tf_op jit(solution)/shard_map/pallas_call | solution.py:122
  55.6 2.1 %shard_map.56 = (f32[1,256]{1,0:T(1,128)S(1)}, f32[1,1024]{1,0:T(1,128)S(1)}, f32[1,1024]{1,0:T(1,128)S(1)}) custom-call(s32[2,512]{1,0:T(2,128)S(1)} %broadcast_in_dim.2.refs_0_, bf16[256,768]{1,0:T(8,128)(2,1)} %collective-permute-done.refs_1_.refs_4_, s32[1,512]{1,0:T(1,128)S(1)} %collective-permute-done.3.refs_2_.refs_7_.refs_8_.refs_9_.refs_10_, ...), custom_call_target="tpu_custom_call" | custom-call | flops 805306368 | bytes 3538944 | tf_op jit(solution)/shard_map/pallas_call | solution.py:122
  57.8 3.6 %shard_map.57 = (f32[1,256]{1,0:T(1,128)S(1)}, f32[1,256]{1,0:T(1,128)S(1)}, f32[1,256]{1,0:T(1,128)S(1)}, f32[1,256]{1,0:T(1,128)S(1)}, f32[1,512]{1,0:T(1,128)S(1)}, /*index=5*/f32[1,512]{1,0:T(1,128)S(1)}) custom-call(s32[2,512]{1,0:T(2,128)S(1)} %broadcast_in_dim.2.refs_0_, bf16[256,768]{1,0:T(8,128)(2,1)S(1)} %copy-done.4, ...), custom_call_target="tpu_custom_call" | custom-call | flops 1610612736 | bytes 3145728 | tf_op jit(solution)/shard_map/pallas_call | solution.py:122
  61.3 3.0 %shard_map.58 = (f32[1,256]{1,0:T(1,128)S(1)}, f32[1,1024]{1,0:T(1,128)S(1)}, f32[1,1024]{1,0:T(1,128)S(1)}, f32[1,512]{1,0:T(1,128)S(1)}, f32[1,512]{1,0:T(1,128)S(1)}) custom-call(s32[2,512]{1,0:T(2,128)S(1)} %broadcast_in_dim.2.refs_0_, bf16[256,768]{1,0:T(8,128)(2,1)} %collective-permute-done.12.refs_1_.refs_5_, ...), custom_call_target="tpu_custom_call" | custom-call | flops 1207959552 | bytes 5111808 | tf_op jit(solution)/shard_map/pallas_call | solution.py:122
  64.4 2.9 %shard_map.59 = (f32[1,256]{1,0:T(1,128)S(1)}, f32[1,1024]{1,0:T(1,128)S(1)}, f32[1,1024]{1,0:T(1,128)S(1)}, f32[1,512]{1,0:T(1,128)S(1)}, f32[1,512]{1,0:T(1,128)S(1)}) custom-call(s32[2,512]{1,0:T(2,128)S(1)} %broadcast_in_dim.2.refs_0_, bf16[256,768]{1,0:T(8,128)(2,1)S(1)} %collective-permute-done.1.refs_1_.refs_6_, ...), custom_call_target="tpu_custom_call" | custom-call | flops 1207959552 | bytes 5111808 | tf_op jit(solution)/shard_map/pallas_call | solution.py:122
  67.3 4.3 %shard_map.60 = (f32[1,256]{1,0:T(1,128)S(1)}, f32[1,256]{1,0:T(1,128)S(1)}, f32[1,256]{1,0:T(1,128)S(1)}, f32[1,256]{1,0:T(1,128)S(1)}, f32[1,256]{1,0:T(1,128)...) custom-call(s32[2,512]{1,0:T(2,128)S(1)} %broadcast_in_dim.2.refs_0_, ...), custom_call_target="tpu_custom_call" | custom-call | flops 2415919104 | bytes 3932160 | tf_op jit(solution)/shard_map/pallas_call | solution.py:122
  71.6 2.3 %collective-permute-start.16 = (f32[1,512]{1,0:T(1,128)S(1)}, f32[1,512]{1,0:T(1,128)S(1)}, u32[]{:S(2)}, u32[]{:S(2)}) collective-permute-start(f32[1,512]{1,0:T(1,128)S(1)} %pad_maximum_fusion.1), channel_id=1, source_target_pairs={{0,4},{2,6},{8,0},{10,2},{12,8},{14,10},{4,12},{6,14},{1,5},{3,7},... | collective-permute-start | bytes 6152 | tf_op jit(solution)/shard_map/ppermute | solution.py:155
  73.9 0.3 collective-permute-start.17
  74.2 3.6 %shard_map.61 = (f32[1,256]{1,0:T(1,128)S(1)}, f32[1,1024]{1,0:T(1,128)S(1)}, f32[1,1024]{1,0:T(1,128)S(1)}, f32[1,512]{1,0:T(1,128)S(1)}, f32[1,512]{1,0:T(1,12...) custom-call(s32[2,512]{1,0:T(2,128)S(1)} %broadcast_in_dim.2.refs_0_, ...), custom_call_target="tpu_custom_call" | custom-call | flops 1610612736 | bytes 6684672 | tf_op jit(solution)/shard_map/pallas_call | solution.py:122
  77.8 2.8 %shard_map.62 = (f32[1,256]{1,0:T(1,128)S(1)}, f32[1,512]{1,0:T(1,128)S(1)}, f32[1,512]{1,0:T(1,128)S(1)}, f32[1,512]{1,0:T(1,128)S(1)}, f32[1,512]{1,0:T(1,128)S(1)}) custom-call(s32[2,512]{1,0:T(2,128)S(1)} %broadcast_in_dim.2.refs_0_, bf16[256,768]{1,0:T(8,128)(2,1)S(1)} %collective-permute-done.2.refs_1_, s32[1,512]{1,0:T(1,128)S(1)} %collective-permute-done.5.refs_2_, ...), custom_call_target="tpu_custom_call" | custom-call | flops 805306368 | bytes 3538944 | tf_op jit(solution)/shard_map/pallas_call | solution.py:122
  80.6 1.4 %collective-permute-start.14 = (f32[1,2048]{1,0:T(1,128)S(1)}, f32[1,2048]{1,0:T(1,128)S(1)}, u32[]{:S(2)}, u32[]{:S(2)}) collective-permute-start(f32[1,2048]{1,0:T(1,128)S(1)} %pad_maximum_fusion), channel_id=1, source_target_pairs={{0,2},{2,0},{4,6},{6,4},{8,10},{10,8},{12,14},{14,12},{1,3},{3,1},... | collective-permute-start | bytes 24584 | tf_op jit(solution)/shard_map/ppermute | solution.py:158
  82.0 1.1 %shard_map.63 = (f32[1,256]{1,0:T(1,128)S(1)}, f32[1,1024]{1,0:T(1,128)S(1)}, f32[1,1024]{1,0:T(1,128)S(1)}) custom-call(s32[2,512]{1,0:T(2,128)S(1)} %broadcast_in_dim.2.refs_0_, bf16[256,768]{1,0:T(8,128)(2,1)S(1)} %collective-permute-done.2.refs_1_, s32[1,512]{1,0:T(1,128)S(1)} %collective-permute-done.5.refs_2_, ...), custom_call_target="tpu_custom_call" | custom-call | flops 805306368 | bytes 3538944 | tf_op jit(solution)/shard_map/pallas_call | solution.py:122
  83.2 1.4 %collective-permute-start.18 = (f32[1,512]{1,0:T(1,128)S(1)}, f32[1,512]{1,0:T(1,128)S(1)}, u32[]{:S(2)}, u32[]{:S(2)}) collective-permute-start(f32[1,512]{1,0:T(1,128)S(1)} %pad_maximum_fusion.3), channel_id=1, source_target_pairs={{0,8},{2,10},{8,12},{10,14},{12,4},{14,6},{4,0},{6,2},{1,9},{3,11}... | collective-permute-start | bytes 6152 | tf_op jit(solution)/shard_map/ppermute | solution.py:155
  84.6 0.1 collective-permute-start.15
  84.7 2.1 %collective-permute-done.18 = f32[1,512]{1,0:T(1,128)S(1)} collective-permute-done((f32[1,512]{1,0:T(1,128)S(1)}, f32[1,512]{1,0:T(1,128)S(1)}, u32[]{:S(2)}, u32[]{:S(2)}) %collective-permute-start.18) | collective-permute-done | bytes 2080 | tf_op jit(solution)/shard_map/ppermute | solution.py:155
  86.8 0.6 fusion.6
  87.4 0.6 fusion.1
  (30 shorter events, 0.1 us)
Async XLA Ops:
  0.6 1.4 %copy-start = (bf16[1024,768]{1,0:T(8,128)(2,1)S(1)}, bf16[1024,768]{1,0:T(8,128)(2,1)}, u32[]{:S(2)}) copy-start(bf16[1024,768]{1,0:T(8,128)(2,1)} %refs_0_.3) | copy-start | bytes 4718596
  2.0 4.9 %copy-start.7 = (s32[512]{0:T(512)S(1)}, s32[512]{0:T(512)}, u32[]{:S(2)}) copy-start(s32[512]{0:T(512)} %param.5) | copy-start | bytes 6148
  2.0 8.0 %copy-start.1 = (bf16[1024,768]{1,0:T(8,128)(2,1)S(1)}, bf16[1024,768]{1,0:T(8,128)(2,1)}, u32[]{:S(2)}) copy-start(bf16[1024,768]{1,0:T(8,128)(2,1)} %refs_0_.3) | copy-start | bytes 4718596
  3.9 48.4 %collective-permute-start.6 = (bf16[1024,768]{1,0:T(8,128)(2,1)S(1)}, bf16[1024,768]{1,0:T(8,128)(2,1)S(1)}, u32[]{:S(2)}, u32[]{:S(2)}) collective-permute-start(bf16[1024,768]{1,0:T(8,128)(2,1)S(1)} %get-tuple-element.56.refs_5_.refs_3_), channel_id=1, source_target_pairs={{0,1},{1,0},{2,3},{3,2},{4,5},{5,4},{6,7},{7,6},{8,9},{9,8},{10,11... | collective-permute-start | bytes 4718600 | tf_op jit(solution)/shard_map/ppermute | solution.py:161
  4.4 21.1 %collective-permute-start.7 = (bf16[512,768]{1,0:T(8,128)(2,1)S(1)}, bf16[512,768]{1,0:T(8,128)(2,1)}, u32[]{:S(2)}, u32[]{:S(2)}) collective-permute-start(bf16[512,768]{1,0:T(8,128)(2,1)S(1)} %get-tuple-element.57), channel_id=1, source_target_pairs={{0,2},{2,0},{4,6},{6,4},{8,10},{10,8},{12,14},{14,12},{1,3},{3,1},... | collective-permute-start | bytes 2359304 | tf_op jit(solution)/shard_map/ppermute | solution.py:158
  6.9 35.2 %collective-permute-start.9 = (bf16[512,768]{1,0:T(8,128)(2,1)}, bf16[512,768]{1,0:T(8,128)(2,1)}, u32[]{:S(2)}, u32[]{:S(2)}) collective-permute-start(bf16[512,768]{1,0:T(8,128)(2,1)} %get-tuple-element.58), channel_id=1, source_target_pairs={{0,2},{2,0},{4,6},{6,4},{8,10},{10,8},{12,14},{14,12},{1,3},{3,1},... | collective-permute-start | bytes 2359304 | tf_op jit(solution)/shard_map/ppermute | solution.py:158
  6.9 6.1 %collective-permute-start.3 = (s32[1,512]{1,0:T(1,128)S(1)}, s32[1,512]{1,0:T(1,128)S(1)}, u32[]{:S(2)}, u32[]{:S(2)}) collective-permute-start(s32[1,512]{1,0:T(1,128)S(1)} %bitcast.5), channel_id=1, source_target_pairs={{0,8},{2,10},{8,12},{10,14},{12,4},{14,6},{4,0},{6,2},{1,9},{3,11}... | collective-permute-start | bytes 6152 | tf_op jit(solution)/shard_map/ppermute | solution.py:155
  10.1 1.1 %copy-start.2 = (bf16[512,768]{1,0:T(8,128)(2,1)S(1)}, bf16[512,768]{1,0:T(8,128)(2,1)}, u32[]{:S(2)}) copy-start(bf16[512,768]{1,0:T(8,128)(2,1)} %x_ref.5) | copy-start | bytes 2359300
  11.4 17.1 %copy-start.3 = (bf16[256,768]{1,0:T(8,128)(2,1)}, bf16[256,768]{1,0:T(8,128)(2,1)S(1)}, u32[]{:S(2)}) copy-start(bf16[256,768]{1,0:T(8,128)(2,1)S(1)} %shard_map.52.refs_1_) | copy-start | bytes 1179652
  11.4 14.1 %collective-permute-start.11 = (bf16[256,768]{1,0:T(8,128)(2,1)S(1)}, bf16[256,768]{1,0:T(8,128)(2,1)}, u32[]{:S(2)}, u32[]{:S(2)}) collective-permute-start(bf16[256,768]{1,0:T(8,128)(2,1)S(1)} %shard_map.52.refs_1_), channel_id=1, source_target_pairs={{0,8},{2,10},{8,12},{10,14},{12,4},{14,6},{4,0},{6,2},{1,9},{3,11}... | collective-permute-start | bytes 1179656 | tf_op jit(solution)/shard_map/ppermute | solution.py:155
  13.0 9.2 %collective-permute-start.4 = (s32[1,512]{1,0:T(1,128)S(1)}, s32[1,512]{1,0:T(1,128)S(1)}, u32[]{:S(2)}, u32[]{:S(2)}) collective-permute-start(s32[1,512]{1,0:T(1,128)S(1)} %collective-permute-done.3.refs_2_.refs_7_.refs_8_.refs_9_.refs_10_), channel_id=1, source_target_pairs={{0,8},{2,10},{8,12},{10,14},{12,4},{14,6},{4,0},{6,2},{1,9},{3,11}... | collective-permute-start | bytes 6152 | tf_op jit(solution)/shard_map/ppermute | solution.py:155
  22.2 12.1 %collective-permute-start = (bf16[256,768]{1,0:T(8,128)(2,1)S(1)}, bf16[256,768]{1,0:T(8,128)(2,1)}, u32[]{:S(2)}, u32[]{:S(2)}) collective-permute-start(bf16[256,768]{1,0:T(8,128)(2,1)S(1)} %shard_map.50.refs_2_), channel_id=1, source_target_pairs={{0,8},{2,10},{8,12},{10,14},{12,4},{14,6},{4,0},{6,2},{1,9},{3,11}... | collective-permute-start | bytes 1179656 | tf_op jit(solution)/shard_map/ppermute | solution.py:155
  24.7 0.8 copy-start.5
  25.5 32.3 %collective-permute-start.8 = (bf16[512,768]{1,0:T(8,128)(2,1)}, bf16[512,768]{1,0:T(8,128)(2,1)}, u32[]{:S(2)}, u32[]{:S(2)}) collective-permute-start(bf16[512,768]{1,0:T(8,128)(2,1)} %collective-permute-done.7.refs_9_.refs_5_.refs_3_), channel_id=1, source_target_pairs={{0,1},{1,0},{2,3},{3,2},{4,5},{5,4},{6,7},{7,6},{8,9},{9,8},{10,11... | collective-permute-start | bytes 2359304 | tf_op jit(solution)/shard_map/ppermute | solution.py:161
  25.5 19.8 %collective-permute-start.12 = (bf16[256,768]{1,0:T(8,128)(2,1)}, bf16[256,768]{1,0:T(8,128)(2,1)}, u32[]{:S(2)}, u32[]{:S(2)}) collective-permute-start(bf16[256,768]{1,0:T(8,128)(2,1)} %collective-permute-done.11.refs_1_.refs_3_), channel_id=1, source_target_pairs={{0,8},{2,10},{8,12},{10,14},{12,4},{14,6},{4,0},{6,2},{1,9},{3,11}... | collective-permute-start | bytes 1179656 | tf_op jit(solution)/shard_map/ppermute | solution.py:155
  34.3 14.7 %collective-permute-start.1 = (bf16[256,768]{1,0:T(8,128)(2,1)}, bf16[256,768]{1,0:T(8,128)(2,1)S(1)}, u32[]{:S(2)}, u32[]{:S(2)}) collective-permute-start(bf16[256,768]{1,0:T(8,128)(2,1)} %collective-permute-done.refs_1_.refs_4_), channel_id=1, source_target_pairs={{0,8},{2,10},{8,12},{10,14},{12,4},{14,6},{4,0},{6,2},{1,9},{3,11}... | collective-permute-start | bytes 1179656 | tf_op jit(solution)/shard_map/ppermute | solution.py:155
  42.1 25.2 %collective-permute-start.10 = (bf16[512,768]{1,0:T(8,128)(2,1)}, bf16[512,768]{1,0:T(8,128)(2,1)S(1)}, u32[]{:S(2)}, u32[]{:S(2)}) collective-permute-start(bf16[512,768]{1,0:T(8,128)(2,1)} %collective-permute-done.9.refs_13_.refs_7_.refs_5_), channel_id=1, source_target_pairs={{0,1},{1,0},{2,3},{3,2},{4,5},{5,4},{6,7},{7,6},{8,9},{9,8},{10,11... | collective-permute-start | bytes 2359304 | tf_op jit(solution)/shard_map/ppermute | solution.py:161
  42.2 1.0 %copy-start.4 = (bf16[256,768]{1,0:T(8,128)(2,1)S(1)}, bf16[256,768]{1,0:T(8,128)(2,1)}, u32[]{:S(2)}) copy-start(bf16[256,768]{1,0:T(8,128)(2,1)} %copy-done.3) | copy-start | bytes 1179652
  43.2 1.0 %copy-start.6 = (bf16[256,768]{1,0:T(8,128)(2,1)S(1)}, bf16[256,768]{1,0:T(8,128)(2,1)}, u32[]{:S(2)}) copy-start(bf16[256,768]{1,0:T(8,128)(2,1)} %copy-done.5) | copy-start | bytes 1179652
  45.4 28.9 %collective-permute-start.5 = (s32[1,512]{1,0:T(1,128)S(1)}, s32[1,512]{1,0:T(1,128)S(1)}, u32[]{:S(2)}, u32[]{:S(2)}) collective-permute-start(s32[1,512]{1,0:T(1,128)S(1)} %collective-permute-done.4.refs_2_.refs_11_.refs_12_), channel_id=1, source_target_pairs={{0,8},{2,10},{8,12},{10,14},{12,4},{14,6},{4,0},{6,2},{1,9},{3,11}... | collective-permute-start | bytes 6152 | tf_op jit(solution)/shard_map/ppermute | solution.py:155
  49.1 25.2 %collective-permute-start.13 = (bf16[256,768]{1,0:T(8,128)(2,1)}, bf16[256,768]{1,0:T(8,128)(2,1)S(1)}, u32[]{:S(2)}, u32[]{:S(2)}) collective-permute-start(bf16[256,768]{1,0:T(8,128)(2,1)} %collective-permute-done.12.refs_1_.refs_5_), channel_id=1, source_target_pairs={{0,8},{2,10},{8,12},{10,14},{12,4},{14,6},{4,0},{6,2},{1,9},{3,11}... | collective-permute-start | bytes 1179656 | tf_op jit(solution)/shard_map/ppermute | solution.py:155
  52.4 25.5 %collective-permute-start.2 = (bf16[256,768]{1,0:T(8,128)(2,1)S(1)}, bf16[256,768]{1,0:T(8,128)(2,1)S(1)}, u32[]{:S(2)}, u32[]{:S(2)}) collective-permute-start(bf16[256,768]{1,0:T(8,128)(2,1)S(1)} %collective-permute-done.1.refs_1_.refs_6_), channel_id=1, source_target_pairs={{0,8},{2,10},{8,12},{10,14},{12,4},{14,6},{4,0},{6,2},{1,9},{3,11}... | collective-permute-start | bytes 1179656 | tf_op jit(solution)/shard_map/ppermute | solution.py:155
  71.6 13.1 %collective-permute-start.16 = (f32[1,512]{1,0:T(1,128)S(1)}, f32[1,512]{1,0:T(1,128)S(1)}, u32[]{:S(2)}, u32[]{:S(2)}) collective-permute-start(f32[1,512]{1,0:T(1,128)S(1)} %pad_maximum_fusion.1), channel_id=1, source_target_pairs={{0,4},{2,6},{8,0},{10,2},{12,8},{14,10},{4,12},{6,14},{1,5},{3,7},... | collective-permute-start | bytes 6152 | tf_op jit(solution)/shard_map/ppermute | solution.py:155
  73.9 10.8 %collective-permute-start.17 = (f32[1,512]{1,0:T(1,128)S(1)}, f32[1,512]{1,0:T(1,128)S(1)}, u32[]{:S(2)}, u32[]{:S(2)}) collective-permute-start(f32[1,512]{1,0:T(1,128)S(1)} %pad_maximum_fusion.2), channel_id=1, source_target_pairs={{0,12},{2,14},{8,4},{10,6},{12,0},{14,2},{4,8},{6,10},{1,13},{3,15... | collective-permute-start | bytes 6152 | tf_op jit(solution)/shard_map/ppermute | solution.py:155
  80.6 4.0 %collective-permute-start.14 = (f32[1,2048]{1,0:T(1,128)S(1)}, f32[1,2048]{1,0:T(1,128)S(1)}, u32[]{:S(2)}, u32[]{:S(2)}) collective-permute-start(f32[1,2048]{1,0:T(1,128)S(1)} %pad_maximum_fusion), channel_id=1, source_target_pairs={{0,2},{2,0},{4,6},{6,4},{8,10},{10,8},{12,14},{14,12},{1,3},{3,1},... | collective-permute-start | bytes 24584 | tf_op jit(solution)/shard_map/ppermute | solution.py:158
  83.2 3.6 %collective-permute-start.18 = (f32[1,512]{1,0:T(1,128)S(1)}, f32[1,512]{1,0:T(1,128)S(1)}, u32[]{:S(2)}, u32[]{:S(2)}) collective-permute-start(f32[1,512]{1,0:T(1,128)S(1)} %pad_maximum_fusion.3), channel_id=1, source_target_pairs={{0,8},{2,10},{8,12},{10,14},{12,4},{14,6},{4,0},{6,2},{1,9},{3,11}... | collective-permute-start | bytes 6152 | tf_op jit(solution)/shard_map/ppermute | solution.py:155
  84.6 2.8 %collective-permute-start.15 = (f32[1,1024]{1,0:T(1,128)S(1)}, f32[1,1024]{1,0:T(1,128)S(1)}, u32[]{:S(2)}, u32[]{:S(2)}) collective-permute-start(f32[1,1024]{1,0:T(1,128)S(1)} %slice_add_fusion), channel_id=1, source_target_pairs={{0,1},{1,0},{2,3},{3,2},{4,5},{5,4},{6,7},{7,6},{8,9},{9,8},{10,11... | collective-permute-start | bytes 12296 | tf_op jit(solution)/shard_map/ppermute | solution.py:161

commit v2 on v1

--- a/solution.py
+++ b/solution.py
@@ -25,26 +25,43 @@
 FIRST = 8
 
 
-def unit_body(parts, n_more, x_ref, *refs):
-    for part, o_ref in zip(parts, refs[n_more:]):
-        values = x_ref[part, :].astype(jnp.float32)
-        squares = jnp.sum(values * values, axis=-1, keepdims=True) + epsilon
-        o_ref[...] = (values * lax.rsqrt(squares)).astype(jnp.bfloat16)
-
-
-def unit_rows_call(rows, parts, more):
+def unit(values):
+    values = values.astype(jnp.float32)
+    squares = jnp.sum(values * values, axis=-1, keepdims=True) + epsilon
+    return (values * lax.rsqrt(squares)).astype(jnp.bfloat16)
+
+
+def unit_body(pieces, outs, x_ref, *refs):
+    o_refs, raw_ref, sem = refs[: len(outs)], refs[-2], refs[-1]
+    copies = [
+        pltpu.make_async_copy(x_ref.at[piece], raw_ref.at[piece], sem.at[k]) for k, piece in enumerate(pieces)
+    ]
+    for copy in copies:
+        copy.start()
+    for copy, piece in zip(copies, pieces):
+        copy.wait()
+        rows = unit(raw_ref[piece, :])
+        for o_ref, out in zip(o_refs, outs):
+            if out.start <= piece.start and piece.stop <= out.stop:
+                o_ref[piece.start - out.start : piece.stop - out.start, :] = rows
+
+
+def unit_rows_call(rows, pieces, outs):
     columns = rows.shape[1]
-    sizes = [part.stop - part.start for part in parts]
-    return pl.pallas_call(
-        functools.partial(unit_body, parts, len(more)),
-        in_specs=[VMEM] * (1 + len(more)),
-        out_specs=[VMEM] * len(parts),
-        out_shape=[pltpu.VMEM((size, columns), jnp.bfloat16) for size in sizes],
-        compiler_params=pltpu.CompilerParams(vmem_limit_bytes=24 * 2**20),
-        cost_estimate=pl.CostEstimate(
-            flops=sum(sizes) * columns * 300, bytes_accessed=sum(sizes) * columns * 4, transcendentals=sum(sizes)
-        ),
-    )(rows, *more)
+    sizes = [out.stop - out.start for out in outs]
+    return list(
+        pl.pallas_call(
+            functools.partial(unit_body, pieces, outs),
+            in_specs=[pl.BlockSpec(memory_space=pltpu.HBM)],
+            out_specs=[VMEM] * len(outs),
+            out_shape=[pltpu.VMEM((size, columns), jnp.bfloat16) for size in sizes],
+            scratch_shapes=[pltpu.VMEM(rows.shape, jnp.bfloat16), pltpu.SemaphoreType.DMA((len(pieces),))],
+            compiler_params=pltpu.CompilerParams(vmem_limit_bytes=24 * 2**20),
+            cost_estimate=pl.CostEstimate(
+                flops=rows.size * 300, bytes_accessed=rows.size * 4, transcendentals=rows.shape[0]
+            ),
+        )(pltpu.with_memory_space_constraint(rows, pltpu.HBM))
+    )
 
 
 def sums_body(n_docs, n_res, cycle, cuts, sides, doc_in, res_in, *refs):
@@ -133,7 +150,7 @@
 
 
 def line_order(count):
-    return list(range(0, count, 2)) + list(reversed(range(1, count, 2)))
+    return [0] + list(range(1, count, 2)) + list(reversed(range(2, count, 2)))
 
 
 def dense(resident, ingest, cluster_ids):
@@ -164,7 +181,7 @@
     place = jnp.stack([here, here ^ 1]).astype(jnp.int32)
     place = jnp.broadcast_to(place[:, None], (2, count))
 
-    own = [unit_rows_call(ingest, [parts[k]], [resident])[0] for k in range(2)]
+    own = unit_rows_call(ingest, parts, parts)
     units = [own]
     owners = [(cluster_ids // CL_OWN).reshape(1, count)]
     for d in range(1, lines):
@@ -175,7 +192,8 @@
     rows = resident.shape[0]
     whole = slice(0, rows)
     halves = [slice(0, rows // 2), slice(rows // 2, rows)]
-    r0, *r0_halves = unit_rows_call(resident, [whole, *halves], [])
+    quarters = [slice(k * rows // 4, (k + 1) * rows // 4) for k in range(4)]
+    r0, *r0_halves = unit_rows_call(resident, quarters, [whole, *halves])
     r2 = [mate(r0_halves[k]) for k in range(2)]
     r1 = twin(r0)
     r3 = [twin(r2[k]) for k in range(2)]
@@ -201,13 +219,12 @@
     d, ab = sums(chunks[0] + chunks[1] + chunks[2], rb, [1, 1], d_own + d1 + d2, [None] * 2)
     d_own, d1, d2 = d[:2], d[2:4], d[4:]
     d3a, a = sums(chunks[3][:1], [r0, r1, *ra, *rb], [0, 0, 1, 1, 1, 1], [None], a + ab)
-    d3b, am = sums(chunks[3][1:], ra + rb, [1] * 4, [None], a[2:])
-    to_mate = jnp.concatenate([am[0], am[2], am[1], am[3]], axis=1)
+    d3b, (s0, s1, s2a, s3a, s2b, s3b) = sums(chunks[3][1:], [r0, r1, *ra, *rb], [0, 0, 1, 1, 1, 1], [None], a)
+    to_twin = jnp.concatenate([s1, s3a, s3b], axis=1)
+    from_twin = twin(to_twin)
+    to_mate = jnp.concatenate([s2a, s2b], axis=1) + from_twin[:, rows:]
     from_mate = mate(to_mate)
-    d3b, an = sums(chunks[3][1:], [r0, r1], [0, 0], d3b, a[:2])
-    to_twin = an[1] + from_mate[:, rows:]
-    from_twin = twin(to_twin)
-    resident_density = an[0] + from_mate[:, :rows] + from_twin
+    resident_density = s0 + from_twin[:, :rows] + from_mate
 
     ingest_density = jnp.concatenate(d_own, axis=1)
     for d, pieces in ((1, d1), (2, d2), (3, d3a + d3b)):

time: 88.6 us -> 88.5 us (level)
  waiting for transfers between devices: 20.7 us -> 27 us
  starting transfers between devices: 29.9 us -> 23.8 us
  local copies, waits for them, and re-layouts: 5.38 us -> 3.59 us
  Pallas kernels: 30 us -> 31.5 us
    ppermute x12, starting transfers between devices: 25.3 us -> 18.9 us  [along(): return lax.ppermute(value, 'blk', pairs)]
    ppermute x3, waiting for transfers between devices: 4.37 us -> 10.3 us  [mate(): return lax.ppermute(value, 'blk', [(p, p ^ 1) for p in range(cycle)])]
    unnamed x16 -> x12, local copies, waits for them, and re-layouts: 5.3 us -> 3.52 us
    pallas_call x3 -> x2, Pallas kernels: 2.19 us -> 3.9 us  [unit_rows_call(): pl.pallas_call(functools.partial(unit_body, pieces, outs), in_specs=[pl.B...]
    ppermute x4, waiting for transfers between devices: 0.01 us -> 1.09 us  [twin(): return lax.ppermute(value, 'rep', [(0, 1), (1, 0)])]
    pallas_call x11 -> x10, Pallas kernels: 27.8 us -> 27.6 us  [kernel_sums(): pl.pallas_call(functools.partial(sums_body, len(docs), len(res), cycle, c...]
  transfers between devices with their start and end apart: 19 -> 19, of which waited for: 5 -> 8; matrix products, arithmetic and copies ran while one was open for 1% -> 1% of each run, Pallas kernels for 32% -> 33%
where the time goes in v2:
time: 88.5 us; the launch traced here: 88 us
  Pallas kernels  31.5 us (36%)
  waiting for transfers between devices  27 us (31%)
  starting transfers between devices  23.8 us (27%)
  local copies, waits for them, and re-layouts  3.59 us (4%)
  other arithmetic  1.32 us (1%)
    pallas_call x10, Pallas kernels, kernel_sums(): pl.pallas_call(functools.partial(sums_body, len(docs), len(res), cycle, c...  27.6 us
    ppermute x12, starting transfers between devices, along(): return lax.ppermute(value, 'blk', pairs)  18.9 us
    ppermute x12, waiting for transfers between devices, along(): return lax.ppermute(value, 'blk', pairs)  15.6 us
    ppermute x3, waiting for transfers between devices, mate(): return lax.ppermute(value, 'blk', [(p, p ^ 1) for p in range(cycle)])  10.3 us
    ppermute x3, starting transfers between devices, mate(): return lax.ppermute(value, 'blk', [(p, p ^ 1) for p in range(cycle)])  4.24 us
    pallas_call x2, Pallas kernels, unit_rows_call(): pl.pallas_call(functools.partial(unit_body, pieces, outs), in_specs=[pl.B...  3.9 us
    unnamed x12, local copies, waits for them, and re-layouts  3.52 us
  transfers between devices with their start and end apart: 19, of which 8 were waited for; matrix products, arithmetic and copies ran while one was open for 1% of the time, Pallas kernels for 33%

profile of v2, /device:TPU:0, one launch (start us, length us, event | category | flops | bytes accessed | tf_op | source)
XLA Modules:
  0.0 88.0 jit_solution(5374202460416432532)
XLA Ops:
  0.6 2.6 %shard_map.51 = (bf16[1024,768]{1,0:T(8,128)(2,1)S(1)}, bf16[512,768]{1,0:T(8,128)(2,1)S(1)}, bf16[512,768]{1,0:T(8,128)(2,1)}) custom-call(bf16[1024,768]{1,0:T(8,128)(2,1)} %x_ref.3), custom_call_target="tpu_custom_call" | custom-call | flops 235929600 | bytes 3145728 | tf_op jit(solution)/shard_map/pallas_call | solution.py:53
  3.2 0.6 collective-permute-start.6
  3.8 2.6 %collective-permute-start.7 = (bf16[512,768]{1,0:T(8,128)(2,1)S(1)}, bf16[512,768]{1,0:T(8,128)(2,1)}, u32[]{:S(2)}, u32[]{:S(2)}) collective-permute-start(bf16[512,768]{1,0:T(8,128)(2,1)S(1)} %get-tuple-element.59), channel_id=1, source_target_pairs={{0,2},{2,0},{4,6},{6,4},{8,10},{10,8},{12,14},{14,12},{1,3},{3,1},... | collective-permute-start | bytes 2359304 | tf_op jit(solution)/shard_map/ppermute | solution.py:175
  6.4 0.1 collective-permute-start.9
  6.4 2.1 %collective-permute-start.3 = (s32[1,512]{1,0:T(1,128)S(1)}, s32[1,512]{1,0:T(1,128)S(1)}, u32[]{:S(2)}, u32[]{:S(2)}) collective-permute-start(s32[1,512]{1,0:T(1,128)S(1)} %bitcast.5), channel_id=1, source_target_pairs={{0,4},{2,6},{4,12},{6,14},{12,8},{14,10},{8,0},{10,2},{1,5},{3,7},... | collective-permute-start | bytes 6152 | tf_op jit(solution)/shard_map/ppermute | solution.py:172
  8.5 2.6 %collective-permute-done.3.refs_2_.refs_7_.refs_8_.refs_9_.refs_10_ = s32[1,512]{1,0:T(1,128)S(1)} collective-permute-done((s32[1,512]{1,0:T(1,128)S(1)}, s32[1,512]{1,0:T(1,128)S(1)}, u32[]{:S(2)}, u32[]{:S(2)}) %collective-permute-start.3) | collective-permute-done | bytes 2080 | tf_op jit(solution)/shard_map/ppermute | solution.py:172
  11.1 1.3 %collective-permute-start.4 = (s32[1,512]{1,0:T(1,128)S(1)}, s32[1,512]{1,0:T(1,128)S(1)}, u32[]{:S(2)}, u32[]{:S(2)}) collective-permute-start(s32[1,512]{1,0:T(1,128)S(1)} %collective-permute-done.3.refs_2_.refs_7_.refs_8_.refs_9_.refs_10_), channel_id=1, source_target_pairs={{0,4},{2,6},{4,12},{6,14},{12,8},{14,10},{8,0},{10,2},{1,5},{3,7},... | collective-permute-start | bytes 6152 | tf_op jit(solution)/shard_map/ppermute | solution.py:172
  12.4 1.3 %shard_map.50 = (bf16[256,768]{1,0:T(8,128)(2,1)S(1)}, bf16[256,768]{1,0:T(8,128)(2,1)S(1)}) custom-call(bf16[512,768]{1,0:T(8,128)(2,1)} %x_ref.2), custom_call_target="tpu_custom_call" | custom-call | flops 117964800 | bytes 1572864 | tf_op jit(solution)/shard_map/pallas_call | solution.py:53
  13.7 3.2 %collective-permute-start.11 = (bf16[256,768]{1,0:T(8,128)(2,1)S(1)}, bf16[256,768]{1,0:T(8,128)(2,1)}, u32[]{:S(2)}, u32[]{:S(2)}) collective-permute-start(bf16[256,768]{1,0:T(8,128)(2,1)S(1)} %get-tuple-element.61.refs_1_), channel_id=1, source_target_pairs={{0,4},{2,6},{4,12},{6,14},{12,8},{14,10},{8,0},{10,2},{1,5},{3,7},... | collective-permute-start | bytes 1179656 | tf_op jit(solution)/shard_map/ppermute | solution.py:172
  17.0 0.8 copy-done
  17.7 0.0 collective-permute-done.4.refs_2_.refs_11_.refs_12_
  17.7 0.0 collective-permute-start
  17.8 0.8 copy-done.2
  18.5 6.3 %collective-permute-done.7.refs_9_.refs_5_ = bf16[512,768]{1,0:T(8,128)(2,1)} collective-permute-done((bf16[512,768]{1,0:T(8,128)(2,1)S(1)}, bf16[512,768]{1,0:T(8,128)(2,1)}, u32[]{:S(2)}, u32[]{:S(2)}) %collective-permute-start.7) | collective-permute-done | bytes 786464 | tf_op jit(solution)/shard_map/ppermute | solution.py:175
  24.8 0.0 collective-permute-start.8
  24.9 1.9 %collective-permute-done.11.refs_1_.refs_3_ = bf16[256,768]{1,0:T(8,128)(2,1)} collective-permute-done((bf16[256,768]{1,0:T(8,128)(2,1)S(1)}, bf16[256,768]{1,0:T(8,128)(2,1)}, u32[]{:S(2)}, u32[]{:S(2)}) %collective-permute-start.11) | collective-permute-done | bytes 393248 | tf_op jit(solution)/shard_map/ppermute | solution.py:172
  26.8 2.3 %collective-permute-start.12 = (bf16[256,768]{1,0:T(8,128)(2,1)}, bf16[256,768]{1,0:T(8,128)(2,1)}, u32[]{:S(2)}, u32[]{:S(2)}) collective-permute-start(bf16[256,768]{1,0:T(8,128)(2,1)} %collective-permute-done.11.refs_1_.refs_3_), channel_id=1, source_target_pairs={{0,4},{2,6},{4,12},{6,14},{12,8},{14,10},{8,0},{10,2},{1,5},{3,7},... | collective-permute-start | bytes 1179656 | tf_op jit(solution)/shard_map/ppermute | solution.py:172
  29.1 6.1 %collective-permute-done.refs_1_.refs_4_ = bf16[256,768]{1,0:T(8,128)(2,1)} collective-permute-done((bf16[256,768]{1,0:T(8,128)(2,1)S(1)}, bf16[256,768]{1,0:T(8,128)(2,1)}, u32[]{:S(2)}, u32[]{:S(2)}) %collective-permute-start) | collective-permute-done | bytes 393248 | tf_op jit(solution)/shard_map/ppermute | solution.py:172
  35.2 2.3 %collective-permute-start.1 = (bf16[256,768]{1,0:T(8,128)(2,1)}, bf16[256,768]{1,0:T(8,128)(2,1)S(1)}, u32[]{:S(2)}, u32[]{:S(2)}) collective-permute-start(bf16[256,768]{1,0:T(8,128)(2,1)} %collective-permute-done.refs_1_.refs_4_), channel_id=1, source_target_pairs={{0,4},{2,6},{4,12},{6,14},{12,8},{14,10},{8,0},{10,2},{1,5},{3,7},... | collective-permute-start | bytes 1179656 | tf_op jit(solution)/shard_map/ppermute | solution.py:172
  37.5 4.0 %collective-permute-done.9.refs_13_.refs_7_ = bf16[512,768]{1,0:T(8,128)(2,1)} collective-permute-done((bf16[512,768]{1,0:T(8,128)(2,1)}, bf16[512,768]{1,0:T(8,128)(2,1)}, u32[]{:S(2)}, u32[]{:S(2)}) %collective-permute-start.9) | collective-permute-done | bytes 786464 | tf_op jit(solution)/shard_map/ppermute | solution.py:175
  41.4 0.0 collective-permute-start.10
  41.4 0.1 pad_add_fusion
  41.5 0.1 broadcast_in_dim.2.refs_0_
  41.6 1.0 %copy-done.1 = bf16[256,768]{1,0:T(8,128)(2,1)S(1)} copy-done((bf16[256,768]{1,0:T(8,128)(2,1)S(1)}, bf16[256,768]{1,0:T(8,128)(2,1)}, u32[]{:S(2)}) %copy-start.1) | copy-done | bytes 393240
  42.6 1.0 %copy-done.3 = bf16[256,768]{1,0:T(8,128)(2,1)S(1)} copy-done((bf16[256,768]{1,0:T(8,128)(2,1)S(1)}, bf16[256,768]{1,0:T(8,128)(2,1)}, u32[]{:S(2)}) %copy-start.3) | copy-done | bytes 393240
  43.6 1.1 %shard_map.52 = (f32[1,256]{1,0:T(1,128)S(1)}, f32[1,256]{1,0:T(1,128)S(1)}, f32[1,1024]{1,0:T(1,128)S(1)}) custom-call(s32[2,512]{1,0:T(2,128)S(1)} %broadcast_in_dim.2.refs_0_, bf16[256,768]{1,0:T(8,128)(2,1)S(1)} %copy-done.1, bf16[256,768]{1,0:T(8,128)(2,1)S(1)} %copy-done.3, s32[1,512]{1,0:T(1,128)S(1)} %bitcast.6, s32[1,512]{1,0:T(1,128)S(1)} %bitcast.7, ...), custom_call_target="tpu_custom_call" | custom-call | flops 805306368 | bytes 2359296 | tf_op jit(solution)/shard_map/pallas_call | solution.py:139
  44.7 1.9 %collective-permute-start.5 = (s32[1,512]{1,0:T(1,128)S(1)}, s32[1,512]{1,0:T(1,128)S(1)}, u32[]{:S(2)}, u32[]{:S(2)}) collective-permute-start(s32[1,512]{1,0:T(1,128)S(1)} %collective-permute-done.4.refs_2_.refs_11_.refs_12_), channel_id=1, source_target_pairs={{0,4},{2,6},{4,12},{6,14},{12,8},{14,10},{8,0},{10,2},{1,5},{3,7},... | collective-permute-start | bytes 6152 | tf_op jit(solution)/shard_map/ppermute | solution.py:172
  46.6 3.2 %collective-permute-done.1.refs_1_.refs_6_ = bf16[256,768]{1,0:T(8,128)(2,1)S(1)} collective-permute-done((bf16[256,768]{1,0:T(8,128)(2,1)}, bf16[256,768]{1,0:T(8,128)(2,1)S(1)}, u32[]{:S(2)}, u32[]{:S(2)}) %collective-permute-start.1) | collective-permute-done | bytes 393248 | tf_op jit(solution)/shard_map/ppermute | solution.py:172
  49.8 2.0 %collective-permute-start.13 = (bf16[256,768]{1,0:T(8,128)(2,1)}, bf16[256,768]{1,0:T(8,128)(2,1)S(1)}, u32[]{:S(2)}, u32[]{:S(2)}) collective-permute-start(bf16[256,768]{1,0:T(8,128)(2,1)} %collective-permute-done.12.refs_1_.refs_5_), channel_id=1, source_target_pairs={{0,4},{2,6},{4,12},{6,14},{12,8},{14,10},{8,0},{10,2},{1,5},{3,7},... | collective-permute-start | bytes 1179656 | tf_op jit(solution)/shard_map/ppermute | solution.py:172
  51.7 1.2 %collective-permute-start.2 = (bf16[256,768]{1,0:T(8,128)(2,1)S(1)}, bf16[256,768]{1,0:T(8,128)(2,1)S(1)}, u32[]{:S(2)}, u32[]{:S(2)}) collective-permute-start(bf16[256,768]{1,0:T(8,128)(2,1)S(1)} %collective-permute-done.1.refs_1_.refs_6_), channel_id=1, source_target_pairs={{0,4},{2,6},{4,12},{6,14},{12,8},{14,10},{8,0},{10,2},{1,5},{3,7},... | collective-permute-start | bytes 1179656 | tf_op jit(solution)/shard_map/ppermute | solution.py:172
  52.9 1.1 %shard_map.53 = (f32[1,256]{1,0:T(1,128)S(1)}, f32[1,256]{1,0:T(1,128)S(1)}, f32[1,1024]{1,0:T(1,128)S(1)}) custom-call(s32[2,512]{1,0:T(2,128)S(1)} %broadcast_in_dim.2.refs_0_, bf16[256,768]{1,0:T(8,128)(2,1)S(1)} %copy-done.1, bf16[256,768]{1,0:T(8,128)(2,1)S(1)} %copy-done.3, s32[1,512]{1,0:T(1,128)S(1)} %bitcast.8, s32[1,512]{1,0:T(1,128)S(1)} %bitcast.9, ...), custom_call_target="tpu_custom_call" | custom-call | flops 805306368 | bytes 2359296 | tf_op jit(solution)/shard_map/pallas_call | solution.py:139
  54.1 2.1 %shard_map.54 = (f32[1,256]{1,0:T(1,128)S(1)}, f32[1,1024]{1,0:T(1,128)S(1)}, f32[1,1024]{1,0:T(1,128)S(1)}) custom-call(s32[2,512]{1,0:T(2,128)S(1)} %broadcast_in_dim.2.refs_0_, bf16[256,768]{1,0:T(8,128)(2,1)} %collective-permute-done.11.refs_1_.refs_3_, s32[1,512]{1,0:T(1,128)S(1)} %collective-permute-done.3.refs_2_.refs_7_.refs_8_.refs_9_.refs_10_, ...), custom_call_target="tpu_custom_call" | custom-call | flops 805306368 | bytes 3538944 | tf_op jit(solution)/shard_map/pallas_call | solution.py:139
  56.2 2.1 %shard_map.55 = (f32[1,256]{1,0:T(1,128)S(1)}, f32[1,1024]{1,0:T(1,128)S(1)}, f32[1,1024]{1,0:T(1,128)S(1)}) custom-call(s32[2,512]{1,0:T(2,128)S(1)} %broadcast_in_dim.2.refs_0_, bf16[256,768]{1,0:T(8,128)(2,1)} %collective-permute-done.refs_1_.refs_4_, s32[1,512]{1,0:T(1,128)S(1)} %collective-permute-done.3.refs_2_.refs_7_.refs_8_.refs_9_.refs_10_, ...), custom_call_target="tpu_custom_call" | custom-call | flops 805306368 | bytes 3538944 | tf_op jit(solution)/shard_map/pallas_call | solution.py:139
  58.3 3.6 %shard_map.56 = (f32[1,256]{1,0:T(1,128)S(1)}, f32[1,256]{1,0:T(1,128)S(1)}, f32[1,256]{1,0:T(1,128)S(1)}, f32[1,256]{1,0:T(1,128)S(1)}, f32[1,512]{1,0:T(1,128)S(1)}, /*index=5*/f32[1,512]{1,0:T(1,128)S(1)}) custom-call(s32[2,512]{1,0:T(2,128)S(1)} %broadcast_in_dim.2.refs_0_, bf16[256,768]{1,0:T(8,128)(2,1)S(1)} %copy-done.1, ...), custom_call_target="tpu_custom_call" | custom-call | flops 1610612736 | bytes 3145728 | tf_op jit(solution)/shard_map/pallas_call | solution.py:139
  61.9 3.0 %shard_map.57 = (f32[1,256]{1,0:T(1,128)S(1)}, f32[1,1024]{1,0:T(1,128)S(1)}, f32[1,1024]{1,0:T(1,128)S(1)}, f32[1,512]{1,0:T(1,128)S(1)}, f32[1,512]{1,0:T(1,128)S(1)}) custom-call(s32[2,512]{1,0:T(2,128)S(1)} %broadcast_in_dim.2.refs_0_, bf16[256,768]{1,0:T(8,128)(2,1)} %collective-permute-done.12.refs_1_.refs_5_, ...), custom_call_target="tpu_custom_call" | custom-call | flops 1207959552 | bytes 5111808 | tf_op jit(solution)/shard_map/pallas_call | solution.py:139
  65.0 3.0 %shard_map.58 = (f32[1,256]{1,0:T(1,128)S(1)}, f32[1,1024]{1,0:T(1,128)S(1)}, f32[1,1024]{1,0:T(1,128)S(1)}, f32[1,512]{1,0:T(1,128)S(1)}, f32[1,512]{1,0:T(1,128)S(1)}) custom-call(s32[2,512]{1,0:T(2,128)S(1)} %broadcast_in_dim.2.refs_0_, bf16[256,768]{1,0:T(8,128)(2,1)S(1)} %collective-permute-done.1.refs_1_.refs_6_, ...), custom_call_target="tpu_custom_call" | custom-call | flops 1207959552 | bytes 5111808 | tf_op jit(solution)/shard_map/pallas_call | solution.py:139
  67.9 4.3 %shard_map.59 = (f32[1,256]{1,0:T(1,128)S(1)}, f32[1,256]{1,0:T(1,128)S(1)}, f32[1,256]{1,0:T(1,128)S(1)}, f32[1,256]{1,0:T(1,128)S(1)}, f32[1,256]{1,0:T(1,128)...) custom-call(s32[2,512]{1,0:T(2,128)S(1)} %broadcast_in_dim.2.refs_0_, ...), custom_call_target="tpu_custom_call" | custom-call | flops 2415919104 | bytes 3932160 | tf_op jit(solution)/shard_map/pallas_call | solution.py:139
  72.3 2.0 %collective-permute-start.16 = (f32[1,512]{1,0:T(1,128)S(1)}, f32[1,512]{1,0:T(1,128)S(1)}, u32[]{:S(2)}, u32[]{:S(2)}) collective-permute-start(f32[1,512]{1,0:T(1,128)S(1)} %pad_maximum_fusion.1), channel_id=1, source_target_pairs={{0,8},{2,10},{4,0},{6,2},{12,4},{14,6},{8,12},{10,14},{1,9},{3,11}... | collective-permute-start | bytes 6152 | tf_op jit(solution)/shard_map/ppermute | solution.py:172
  74.3 0.6 collective-permute-start.17
  74.9 3.6 %shard_map.60 = (f32[1,256]{1,0:T(1,128)S(1)}, f32[1,1024]{1,0:T(1,128)S(1)}, f32[1,1024]{1,0:T(1,128)S(1)}, f32[1,512]{1,0:T(1,128)S(1)}, f32[1,512]{1,0:T(1,12...) custom-call(s32[2,512]{1,0:T(2,128)S(1)} %broadcast_in_dim.2.refs_0_, ...), custom_call_target="tpu_custom_call" | custom-call | flops 1610612736 | bytes 6684672 | tf_op jit(solution)/shard_map/pallas_call | solution.py:139
  78.5 3.6 %shard_map.61 = (f32[1,256]{1,0:T(1,128)S(1)}, f32[1,1024]{1,0:T(1,128)S(1)}, f32[1,1024]{1,0:T(1,128)S(1)}, f32[1,512]{1,0:T(1,128)S(1)}, f32[1,512]{1,0:T(1,12...) custom-call(s32[2,512]{1,0:T(2,128)S(1)} %broadcast_in_dim.2.refs_0_, ...), custom_call_target="tpu_custom_call" | custom-call | flops 1610612736 | bytes 6684672 | tf_op jit(solution)/shard_map/pallas_call | solution.py:139
  82.1 0.1 collective-permute-start.14
  82.2 0.1 collective-permute-start.18
  82.3 1.1 %collective-permute-done.14 = f32[1,2048]{1,0:T(1,128)S(1)} collective-permute-done((f32[1,2048]{1,0:T(1,128)S(1)}, f32[1,2048]{1,0:T(1,128)S(1)}, u32[]{:S(2)}, u32[]{:S(2)}) %collective-permute-start.14) | collective-permute-done | bytes 8224 | tf_op jit(solution)/shard_map/ppermute | solution.py:178
  83.4 1.6 %collective-permute-start.15 = (f32[1,1024]{1,0:T(1,128)S(1)}, f32[1,1024]{1,0:T(1,128)S(1)}, u32[]{:S(2)}, u32[]{:S(2)}) collective-permute-start(f32[1,1024]{1,0:T(1,128)S(1)} %slice_add_fusion), channel_id=1, source_target_pairs={{0,2},{2,0},{4,6},{6,4},{8,10},{10,8},{12,14},{14,12},{1,3},{3,1},... | collective-permute-start | bytes 12296 | tf_op jit(solution)/shard_map/ppermute | solution.py:175
  85.0 1.8 %collective-permute-done.18 = f32[1,512]{1,0:T(1,128)S(1)} collective-permute-done((f32[1,512]{1,0:T(1,128)S(1)}, f32[1,512]{1,0:T(1,128)S(1)}, u32[]{:S(2)}, u32[]{:S(2)}) %collective-permute-start.18) | collective-permute-done | bytes 2080 | tf_op jit(solution)/shard_map/ppermute | solution.py:172
  86.8 0.6 fusion.6
  87.4 0.6 fusion.1
  (24 shorter events, 0.1 us)
Async XLA Ops:
  0.6 5.8 %copy-start.5 = (s32[512]{0:T(512)S(1)}, s32[512]{0:T(512)}, u32[]{:S(2)}) copy-start(s32[512]{0:T(512)} %param.5) | copy-start | bytes 6148
  3.2 48.5 %collective-permute-start.6 = (bf16[1024,768]{1,0:T(8,128)(2,1)S(1)}, bf16[1024,768]{1,0:T(8,128)(2,1)S(1)}, u32[]{:S(2)}, u32[]{:S(2)}) collective-permute-start(bf16[1024,768]{1,0:T(8,128)(2,1)S(1)} %get-tuple-element.58.refs_5_.refs_3_), channel_id=1, source_target_pairs={{0,1},{1,0},{2,3},{3,2},{4,5},{5,4},{6,7},{7,6},{8,9},{9,8},{10,11... | collective-permute-start | bytes 4718600 | tf_op jit(solution)/shard_map/ppermute | solution.py:178
  3.8 21.1 %collective-permute-start.7 = (bf16[512,768]{1,0:T(8,128)(2,1)S(1)}, bf16[512,768]{1,0:T(8,128)(2,1)}, u32[]{:S(2)}, u32[]{:S(2)}) collective-permute-start(bf16[512,768]{1,0:T(8,128)(2,1)S(1)} %get-tuple-element.59), channel_id=1, source_target_pairs={{0,2},{2,0},{4,6},{6,4},{8,10},{10,8},{12,14},{14,12},{1,3},{3,1},... | collective-permute-start | bytes 2359304 | tf_op jit(solution)/shard_map/ppermute | solution.py:175
  6.4 35.1 %collective-permute-start.9 = (bf16[512,768]{1,0:T(8,128)(2,1)}, bf16[512,768]{1,0:T(8,128)(2,1)}, u32[]{:S(2)}, u32[]{:S(2)}) collective-permute-start(bf16[512,768]{1,0:T(8,128)(2,1)} %get-tuple-element.60), channel_id=1, source_target_pairs={{0,2},{2,0},{4,6},{6,4},{8,10},{10,8},{12,14},{14,12},{1,3},{3,1},... | collective-permute-start | bytes 2359304 | tf_op jit(solution)/shard_map/ppermute | solution.py:175
  6.4 4.6 %collective-permute-start.3 = (s32[1,512]{1,0:T(1,128)S(1)}, s32[1,512]{1,0:T(1,128)S(1)}, u32[]{:S(2)}, u32[]{:S(2)}) collective-permute-start(s32[1,512]{1,0:T(1,128)S(1)} %bitcast.5), channel_id=1, source_target_pairs={{0,4},{2,6},{4,12},{6,14},{12,8},{14,10},{8,0},{10,2},{1,5},{3,7},... | collective-permute-start | bytes 6152 | tf_op jit(solution)/shard_map/ppermute | solution.py:172
  11.1 6.7 %collective-permute-start.4 = (s32[1,512]{1,0:T(1,128)S(1)}, s32[1,512]{1,0:T(1,128)S(1)}, u32[]{:S(2)}, u32[]{:S(2)}) collective-permute-start(s32[1,512]{1,0:T(1,128)S(1)} %collective-permute-done.3.refs_2_.refs_7_.refs_8_.refs_9_.refs_10_), channel_id=1, source_target_pairs={{0,4},{2,6},{4,12},{6,14},{12,8},{14,10},{8,0},{10,2},{1,5},{3,7},... | collective-permute-start | bytes 6152 | tf_op jit(solution)/shard_map/ppermute | solution.py:172
  13.7 13.0 %collective-permute-start.11 = (bf16[256,768]{1,0:T(8,128)(2,1)S(1)}, bf16[256,768]{1,0:T(8,128)(2,1)}, u32[]{:S(2)}, u32[]{:S(2)}) collective-permute-start(bf16[256,768]{1,0:T(8,128)(2,1)S(1)} %get-tuple-element.61.refs_1_), channel_id=1, source_target_pairs={{0,4},{2,6},{4,12},{6,14},{12,8},{14,10},{8,0},{10,2},{1,5},{3,7},... | collective-permute-start | bytes 1179656 | tf_op jit(solution)/shard_map/ppermute | solution.py:172
  17.0 0.8 copy-start
  17.7 17.5 %collective-permute-start = (bf16[256,768]{1,0:T(8,128)(2,1)S(1)}, bf16[256,768]{1,0:T(8,128)(2,1)}, u32[]{:S(2)}, u32[]{:S(2)}) collective-permute-start(bf16[256,768]{1,0:T(8,128)(2,1)S(1)} %get-tuple-element.57.refs_2_), channel_id=1, source_target_pairs={{0,4},{2,6},{4,12},{6,14},{12,8},{14,10},{8,0},{10,2},{1,5},{3,7},... | collective-permute-start | bytes 1179656 | tf_op jit(solution)/shard_map/ppermute | solution.py:172
  17.8 0.8 copy-start.2
  24.8 33.5 %collective-permute-start.8 = (bf16[512,768]{1,0:T(8,128)(2,1)}, bf16[512,768]{1,0:T(8,128)(2,1)}, u32[]{:S(2)}, u32[]{:S(2)}) collective-permute-start(bf16[512,768]{1,0:T(8,128)(2,1)} %collective-permute-done.7.refs_9_.refs_5_), channel_id=1, source_target_pairs={{0,1},{1,0},{2,3},{3,2},{4,5},{5,4},{6,7},{7,6},{8,9},{9,8},{10,11... | collective-permute-start | bytes 2359304 | tf_op jit(solution)/shard_map/ppermute | solution.py:178
  26.8 17.9 %collective-permute-start.12 = (bf16[256,768]{1,0:T(8,128)(2,1)}, bf16[256,768]{1,0:T(8,128)(2,1)}, u32[]{:S(2)}, u32[]{:S(2)}) collective-permute-start(bf16[256,768]{1,0:T(8,128)(2,1)} %collective-permute-done.11.refs_1_.refs_3_), channel_id=1, source_target_pairs={{0,4},{2,6},{4,12},{6,14},{12,8},{14,10},{8,0},{10,2},{1,5},{3,7},... | collective-permute-start | bytes 1179656 | tf_op jit(solution)/shard_map/ppermute | solution.py:172
  35.2 14.5 %collective-permute-start.1 = (bf16[256,768]{1,0:T(8,128)(2,1)}, bf16[256,768]{1,0:T(8,128)(2,1)S(1)}, u32[]{:S(2)}, u32[]{:S(2)}) collective-permute-start(bf16[256,768]{1,0:T(8,128)(2,1)} %collective-permute-done.refs_1_.refs_4_), channel_id=1, source_target_pairs={{0,4},{2,6},{4,12},{6,14},{12,8},{14,10},{8,0},{10,2},{1,5},{3,7},... | collective-permute-start | bytes 1179656 | tf_op jit(solution)/shard_map/ppermute | solution.py:172
  41.4 26.5 %collective-permute-start.10 = (bf16[512,768]{1,0:T(8,128)(2,1)}, bf16[512,768]{1,0:T(8,128)(2,1)S(1)}, u32[]{:S(2)}, u32[]{:S(2)}) collective-permute-start(bf16[512,768]{1,0:T(8,128)(2,1)} %collective-permute-done.9.refs_13_.refs_7_), channel_id=1, source_target_pairs={{0,1},{1,0},{2,3},{3,2},{4,5},{5,4},{6,7},{7,6},{8,9},{9,8},{10,11... | collective-permute-start | bytes 2359304 | tf_op jit(solution)/shard_map/ppermute | solution.py:178
  41.6 1.0 %copy-start.1 = (bf16[256,768]{1,0:T(8,128)(2,1)S(1)}, bf16[256,768]{1,0:T(8,128)(2,1)}, u32[]{:S(2)}) copy-start(bf16[256,768]{1,0:T(8,128)(2,1)} %copy-done) | copy-start | bytes 1179652
  42.6 1.0 %copy-start.3 = (bf16[256,768]{1,0:T(8,128)(2,1)S(1)}, bf16[256,768]{1,0:T(8,128)(2,1)}, u32[]{:S(2)}) copy-start(bf16[256,768]{1,0:T(8,128)(2,1)} %copy-done.2) | copy-start | bytes 1179652
  44.7 30.2 %collective-permute-start.5 = (s32[1,512]{1,0:T(1,128)S(1)}, s32[1,512]{1,0:T(1,128)S(1)}, u32[]{:S(2)}, u32[]{:S(2)}) collective-permute-start(s32[1,512]{1,0:T(1,128)S(1)} %collective-permute-done.4.refs_2_.refs_11_.refs_12_), channel_id=1, source_target_pairs={{0,4},{2,6},{4,12},{6,14},{12,8},{14,10},{8,0},{10,2},{1,5},{3,7},... | collective-permute-start | bytes 6152 | tf_op jit(solution)/shard_map/ppermute | solution.py:172
  49.8 25.2 %collective-permute-start.13 = (bf16[256,768]{1,0:T(8,128)(2,1)}, bf16[256,768]{1,0:T(8,128)(2,1)S(1)}, u32[]{:S(2)}, u32[]{:S(2)}) collective-permute-start(bf16[256,768]{1,0:T(8,128)(2,1)} %collective-permute-done.12.refs_1_.refs_5_), channel_id=1, source_target_pairs={{0,4},{2,6},{4,12},{6,14},{12,8},{14,10},{8,0},{10,2},{1,5},{3,7},... | collective-permute-start | bytes 1179656 | tf_op jit(solution)/shard_map/ppermute | solution.py:172
  51.7 26.8 %collective-permute-start.2 = (bf16[256,768]{1,0:T(8,128)(2,1)S(1)}, bf16[256,768]{1,0:T(8,128)(2,1)S(1)}, u32[]{:S(2)}, u32[]{:S(2)}) collective-permute-start(bf16[256,768]{1,0:T(8,128)(2,1)S(1)} %collective-permute-done.1.refs_1_.refs_6_), channel_id=1, source_target_pairs={{0,4},{2,6},{4,12},{6,14},{12,8},{14,10},{8,0},{10,2},{1,5},{3,7},... | collective-permute-start | bytes 1179656 | tf_op jit(solution)/shard_map/ppermute | solution.py:172
  64.9 3.0 %copy-start.4 = (bf16[256,768]{1,0:T(8,128)(2,1)S(1)}, bf16[256,768]{1,0:T(8,128)(2,1)}, u32[]{:S(2)}) copy-start(bf16[256,768]{1,0:T(8,128)(2,1)} %copy-done.2) | copy-start | bytes 1179652
  72.3 12.7 %collective-permute-start.16 = (f32[1,512]{1,0:T(1,128)S(1)}, f32[1,512]{1,0:T(1,128)S(1)}, u32[]{:S(2)}, u32[]{:S(2)}) collective-permute-start(f32[1,512]{1,0:T(1,128)S(1)} %pad_maximum_fusion.1), channel_id=1, source_target_pairs={{0,8},{2,10},{4,0},{6,2},{12,4},{14,6},{8,12},{10,14},{1,9},{3,11}... | collective-permute-start | bytes 6152 | tf_op jit(solution)/shard_map/ppermute | solution.py:172
  74.3 10.7 %collective-permute-start.17 = (f32[1,512]{1,0:T(1,128)S(1)}, f32[1,512]{1,0:T(1,128)S(1)}, u32[]{:S(2)}, u32[]{:S(2)}) collective-permute-start(f32[1,512]{1,0:T(1,128)S(1)} %pad_maximum_fusion.2), channel_id=1, source_target_pairs={{0,12},{2,14},{4,8},{6,10},{12,0},{14,2},{8,4},{10,6},{1,13},{3,15... | collective-permute-start | bytes 6152 | tf_op jit(solution)/shard_map/ppermute | solution.py:172
  82.1 1.2 %collective-permute-start.14 = (f32[1,2048]{1,0:T(1,128)S(1)}, f32[1,2048]{1,0:T(1,128)S(1)}, u32[]{:S(2)}, u32[]{:S(2)}) collective-permute-start(f32[1,2048]{1,0:T(1,128)S(1)} %pad_maximum_fusion), channel_id=1, source_target_pairs={{0,1},{1,0},{2,3},{3,2},{4,5},{5,4},{6,7},{7,6},{8,9},{9,8},{10,11... | collective-permute-start | bytes 24584 | tf_op jit(solution)/shard_map/ppermute | solution.py:178
  82.2 4.5 %collective-permute-start.18 = (f32[1,512]{1,0:T(1,128)S(1)}, f32[1,512]{1,0:T(1,128)S(1)}, u32[]{:S(2)}, u32[]{:S(2)}) collective-permute-start(f32[1,512]{1,0:T(1,128)S(1)} %pad_maximum_fusion.3), channel_id=1, source_target_pairs={{0,4},{2,6},{4,12},{6,14},{12,8},{14,10},{8,0},{10,2},{1,5},{3,7},... | collective-permute-start | bytes 6152 | tf_op jit(solution)/shard_map/ppermute | solution.py:172
  83.4 4.0 %collective-permute-start.15 = (f32[1,1024]{1,0:T(1,128)S(1)}, f32[1,1024]{1,0:T(1,128)S(1)}, u32[]{:S(2)}, u32[]{:S(2)}) collective-permute-start(f32[1,1024]{1,0:T(1,128)S(1)} %slice_add_fusion), channel_id=1, source_target_pairs={{0,2},{2,0},{4,6},{6,4},{8,10},{10,8},{12,14},{14,12},{1,3},{3,1},... | collective-permute-start | bytes 12296 | tf_op jit(solution)/shard_map/ppermute | solution.py:175

commit v3 on v2

--- a/solution.py
+++ b/solution.py
@@ -149,6 +149,38 @@
     return list(out[: len(docs)]), list(out[len(docs) :])
 
 
+def scores_body(n_res, n_doc, *refs):
+    terms, (res_hbm, doc_hbm, res_ref, doc_ref, sem) = refs[:-5], refs[-5:]
+    res_rows = res_ref.shape[1]
+    total = terms[0][:, :res_rows]
+    for term in terms[1:n_res]:
+        total = total + term[:, :res_rows]
+    res_ref[...] = jnp.log1p(total)
+    first = pltpu.make_async_copy(res_ref, res_hbm, sem.at[0])
+    first.start()
+    total = jnp.concatenate([term[...] for term in terms[n_res : n_res + n_doc]], axis=1)
+    for term in terms[n_res + n_doc :]:
+        total = total + term[...]
+    doc_ref[...] = jnp.log1p(total)
+    second = pltpu.make_async_copy(doc_ref, doc_hbm, sem.at[1])
+    second.start()
+    first.wait()
+    second.wait()
+
+
+def scores_call(rows, count, res_terms, own_terms, doc_terms):
+    shapes = [(1, rows), (1, count)]
+    return pl.pallas_call(
+        functools.partial(scores_body, len(res_terms), len(own_terms)),
+        in_specs=[VMEM] * (len(res_terms) + len(own_terms) + len(doc_terms)),
+        out_specs=[pl.BlockSpec(memory_space=pltpu.HBM)] * 2,
+        out_shape=[jax.ShapeDtypeStruct(shape, jnp.float32) for shape in shapes],
+        scratch_shapes=[pltpu.VMEM(shape, jnp.float32) for shape in shapes] + [pltpu.SemaphoreType.DMA((2,))],
+        name="scores",
+        compiler_params=pltpu.CompilerParams(vmem_limit_bytes=8 * 2**20),
+    )(*res_terms, *own_terms, *doc_terms)
+
+
 def line_order(count):
     return [0] + list(range(1, count, 2)) + list(reversed(range(2, count, 2)))
 
@@ -181,7 +213,7 @@
     place = jnp.stack([here, here ^ 1]).astype(jnp.int32)
     place = jnp.broadcast_to(place[:, None], (2, count))
 
-    own = unit_rows_call(ingest, parts, parts)
+    own = [unit_rows_call(ingest, [parts[k]], [parts[k]])[0] for k in range(2)]
     units = [own]
     owners = [(cluster_ids // CL_OWN).reshape(1, count)]
     for d in range(1, lines):
@@ -224,13 +256,12 @@
     from_twin = twin(to_twin)
     to_mate = jnp.concatenate([s2a, s2b], axis=1) + from_twin[:, rows:]
     from_mate = mate(to_mate)
-    resident_density = s0 + from_twin[:, :rows] + from_mate
-
-    ingest_density = jnp.concatenate(d_own, axis=1)
+    backs = []
     for d, pieces in ((1, d1), (2, d2), (3, d3a + d3b)):
         pieces = jnp.concatenate(pieces, axis=1)
-        ingest_density = ingest_density + along(pieces, -d)
-    return (jnp.log1p(resident_density).reshape(-1), jnp.log1p(ingest_density).reshape(-1))
+        backs.append(along(pieces, -d))
+    res_scores, doc_scores = scores_call(rows, count, [s0, from_twin, from_mate], d_own, backs)
+    return res_scores.reshape(-1), doc_scores.reshape(-1)
 
 
 def shifted(value, axis, steps):

time: 88.5 us -> 87.3 us (0.986)
  Pallas kernels: 31.5 us -> 33 us
  other arithmetic: 1.32 us -> 0.12 us
    ppermute x12, waiting for transfers between devices: 15.6 us -> 18.9 us  [along(): return lax.ppermute(value, 'blk', pairs)]
    ppermute x3, waiting for transfers between devices: 10.3 us -> 7.32 us  [mate(): return lax.ppermute(value, 'blk', [(p, p ^ 1) for p in range(cycle)])]
    log1p x2 -> x0, other arithmetic: 1.21 us -> none  [the longest x1 0.61 us: dense_body(): jnp.log1p(resident_density).reshape(-1)]
    ppermute x4, waiting for transfers between devices: 1.09 us -> 0.01 us  [twin(): return lax.ppermute(value, 'rep', [(0, 1), (1, 0)])]
    pallas_call x2 -> x3, Pallas kernels: 3.9 us -> 4.9 us  [unit_rows_call(): pl.pallas_call(functools.partial(unit_body, pieces, outs), in_specs=[pl.B...]
    unnamed x12 -> x10, local copies, waits for them, and re-layouts: 3.52 us -> 2.75 us
  transfers between devices with their start and end apart: 19 -> 19, of which waited for: 8 -> 6; matrix products, arithmetic and copies ran while one was open for 1% -> 0% of each run, Pallas kernels for 33% -> 30%
where the time goes in v3:
time: 87.3 us; the launch traced here: 86.8 us
  Pallas kernels  33 us (38%)
  waiting for transfers between devices  26.2 us (30%)
  starting transfers between devices  23.6 us (27%)
  local copies, waits for them, and re-layouts  2.82 us (3%)
  between operations  0.93 us (1%)
    pallas_call x10, Pallas kernels, kernel_sums(): pl.pallas_call(functools.partial(sums_body, len(docs), len(res), cycle, c...  27.5 us
    ppermute x12, waiting for transfers between devices, along(): return lax.ppermute(value, 'blk', pairs)  18.9 us
    ppermute x12, starting transfers between devices, along(): return lax.ppermute(value, 'blk', pairs)  18.7 us
    ppermute x3, waiting for transfers between devices, mate(): return lax.ppermute(value, 'blk', [(p, p ^ 1) for p in range(cycle)])  7.32 us
    pallas_call x3, Pallas kernels, unit_rows_call(): pl.pallas_call(functools.partial(unit_body, pieces, outs), in_specs=[pl.B...  4.9 us
    ppermute x3, starting transfers between devices, mate(): return lax.ppermute(value, 'blk', [(p, p ^ 1) for p in range(cycle)])  4.24 us
    unnamed x10, local copies, waits for them, and re-layouts  2.75 us
  transfers between devices with their start and end apart: 19, of which 6 were waited for; matrix products, arithmetic and copies ran while one was open for 0% of the time, Pallas kernels for 30%

profile of v3, /device:TPU:0, one launch (start us, length us, event | category | flops | bytes accessed | tf_op | source)
XLA Modules:
  0.0 86.8 jit_solution(5827075109660167279)
XLA Ops:
  0.6 2.6 %shard_map.51 = (bf16[1024,768]{1,0:T(8,128)(2,1)S(1)}, bf16[512,768]{1,0:T(8,128)(2,1)S(1)}, bf16[512,768]{1,0:T(8,128)(2,1)}) custom-call(bf16[1024,768]{1,0:T(8,128)(2,1)} %x_ref.4), custom_call_target="tpu_custom_call" | custom-call | flops 235929600 | bytes 3145728 | tf_op jit(solution)/shard_map/pallas_call | solution.py:53
  3.2 0.6 collective-permute-start.6
  3.8 2.6 %collective-permute-start.7 = (bf16[512,768]{1,0:T(8,128)(2,1)S(1)}, bf16[512,768]{1,0:T(8,128)(2,1)}, u32[]{:S(2)}, u32[]{:S(2)}) collective-permute-start(bf16[512,768]{1,0:T(8,128)(2,1)S(1)} %get-tuple-element.58), channel_id=1, source_target_pairs={{0,2},{2,0},{4,6},{6,4},{8,10},{10,8},{12,14},{14,12},{1,3},{3,1},... | collective-permute-start | bytes 2359304 | tf_op jit(solution)/shard_map/ppermute | solution.py:207
  6.4 0.1 collective-permute-start.9
  6.4 2.1 %collective-permute-start.3 = (s32[1,512]{1,0:T(1,128)S(1)}, s32[1,512]{1,0:T(1,128)S(1)}, u32[]{:S(2)}, u32[]{:S(2)}) collective-permute-start(s32[1,512]{1,0:T(1,128)S(1)} %bitcast.5), channel_id=1, source_target_pairs={{0,4},{2,6},{4,12},{6,14},{12,8},{14,10},{8,0},{10,2},{1,5},{3,7},... | collective-permute-start | bytes 6152 | tf_op jit(solution)/shard_map/ppermute | solution.py:204
  8.5 1.2 %shard_map.52.refs_1_ = bf16[256,768]{1,0:T(8,128)(2,1)S(1)} custom-call(bf16[512,768]{1,0:T(8,128)(2,1)} %x_ref.5), custom_call_target="tpu_custom_call" | custom-call | flops 117964800 | bytes 1572864 | tf_op jit(solution)/shard_map/pallas_call | solution.py:53
  9.7 2.6 %collective-permute-start.11 = (bf16[256,768]{1,0:T(8,128)(2,1)S(1)}, bf16[256,768]{1,0:T(8,128)(2,1)}, u32[]{:S(2)}, u32[]{:S(2)}) collective-permute-start(bf16[256,768]{1,0:T(8,128)(2,1)S(1)} %shard_map.52.refs_1_), channel_id=1, source_target_pairs={{0,4},{2,6},{4,12},{6,14},{12,8},{14,10},{8,0},{10,2},{1,5},{3,7},... | collective-permute-start | bytes 1179656 | tf_op jit(solution)/shard_map/ppermute | solution.py:204
  12.3 0.0 collective-permute-done.3.refs_2_.refs_7_.refs_8_.refs_9_.refs_10_
  12.3 0.5 collective-permute-start.4
  12.8 1.2 %shard_map.50.refs_2_ = bf16[256,768]{1,0:T(8,128)(2,1)S(1)} custom-call(bf16[512,768]{1,0:T(8,128)(2,1)} %x_ref.5), custom_call_target="tpu_custom_call" | custom-call | flops 117964800 | bytes 1572864 | tf_op jit(solution)/shard_map/pallas_call | solution.py:53
  14.0 7.4 %collective-permute-done.4.refs_2_.refs_11_.refs_12_ = s32[1,512]{1,0:T(1,128)S(1)} collective-permute-done((s32[1,512]{1,0:T(1,128)S(1)}, s32[1,512]{1,0:T(1,128)S(1)}, u32[]{:S(2)}, u32[]{:S(2)}) %collective-permute-start.4) | collective-permute-done | bytes 2080 | tf_op jit(solution)/shard_map/ppermute | solution.py:204
  21.4 1.7 %collective-permute-start = (bf16[256,768]{1,0:T(8,128)(2,1)S(1)}, bf16[256,768]{1,0:T(8,128)(2,1)}, u32[]{:S(2)}, u32[]{:S(2)}) collective-permute-start(bf16[256,768]{1,0:T(8,128)(2,1)S(1)} %shard_map.50.refs_2_), channel_id=1, source_target_pairs={{0,4},{2,6},{4,12},{6,14},{12,8},{14,10},{8,0},{10,2},{1,5},{3,7},... | collective-permute-start | bytes 1179656 | tf_op jit(solution)/shard_map/ppermute | solution.py:204
  23.1 0.7 copy-done.2
  23.8 1.0 %collective-permute-done.7.refs_9_.refs_5_ = bf16[512,768]{1,0:T(8,128)(2,1)} collective-permute-done((bf16[512,768]{1,0:T(8,128)(2,1)S(1)}, bf16[512,768]{1,0:T(8,128)(2,1)}, u32[]{:S(2)}, u32[]{:S(2)}) %collective-permute-start.7) | collective-permute-done | bytes 786464 | tf_op jit(solution)/shard_map/ppermute | solution.py:207
  24.9 0.0 collective-permute-start.8
  24.9 2.1 %collective-permute-start.12 = (bf16[256,768]{1,0:T(8,128)(2,1)}, bf16[256,768]{1,0:T(8,128)(2,1)}, u32[]{:S(2)}, u32[]{:S(2)}) collective-permute-start(bf16[256,768]{1,0:T(8,128)(2,1)} %collective-permute-done.11.refs_1_.refs_3_), channel_id=1, source_target_pairs={{0,4},{2,6},{4,12},{6,14},{12,8},{14,10},{8,0},{10,2},{1,5},{3,7},... | collective-permute-start | bytes 1179656 | tf_op jit(solution)/shard_map/ppermute | solution.py:204
  26.9 7.4 %collective-permute-done.refs_1_.refs_4_ = bf16[256,768]{1,0:T(8,128)(2,1)} collective-permute-done((bf16[256,768]{1,0:T(8,128)(2,1)S(1)}, bf16[256,768]{1,0:T(8,128)(2,1)}, u32[]{:S(2)}, u32[]{:S(2)}) %collective-permute-start) | collective-permute-done | bytes 393248 | tf_op jit(solution)/shard_map/ppermute | solution.py:204
  34.4 0.8 collective-permute-start.1
  35.2 6.3 %collective-permute-done.9.refs_13_.refs_7_ = bf16[512,768]{1,0:T(8,128)(2,1)} collective-permute-done((bf16[512,768]{1,0:T(8,128)(2,1)}, bf16[512,768]{1,0:T(8,128)(2,1)}, u32[]{:S(2)}, u32[]{:S(2)}) %collective-permute-start.9) | collective-permute-done | bytes 786464 | tf_op jit(solution)/shard_map/ppermute | solution.py:207
  41.4 0.0 collective-permute-start.10
  41.5 0.1 pad_add_fusion
  41.5 0.1 broadcast_in_dim.2.refs_0_
  41.6 1.0 %copy-done.1 = bf16[256,768]{1,0:T(8,128)(2,1)S(1)} copy-done((bf16[256,768]{1,0:T(8,128)(2,1)S(1)}, bf16[256,768]{1,0:T(8,128)(2,1)}, u32[]{:S(2)}) %copy-start.1) | copy-done | bytes 393240
  42.6 1.0 %copy-done.3 = bf16[256,768]{1,0:T(8,128)(2,1)S(1)} copy-done((bf16[256,768]{1,0:T(8,128)(2,1)S(1)}, bf16[256,768]{1,0:T(8,128)(2,1)}, u32[]{:S(2)}) %copy-start.3) | copy-done | bytes 393240
  43.6 1.1 %shard_map.53 = (f32[1,256]{1,0:T(1,128)S(1)}, f32[1,256]{1,0:T(1,128)S(1)}, f32[1,1024]{1,0:T(1,128)S(1)}) custom-call(s32[2,512]{1,0:T(2,128)S(1)} %broadcast_in_dim.2.refs_0_, bf16[256,768]{1,0:T(8,128)(2,1)S(1)} %copy-done.1, bf16[256,768]{1,0:T(8,128)(2,1)S(1)} %copy-done.3, s32[1,512]{1,0:T(1,128)S(1)} %bitcast.6, s32[1,512]{1,0:T(1,128)S(1)} %bitcast.7, ...), custom_call_target="tpu_custom_call" | custom-call | flops 805306368 | bytes 2359296 | tf_op jit(solution)/shard_map/pallas_call | solution.py:139
  44.7 1.9 %collective-permute-start.5 = (s32[1,512]{1,0:T(1,128)S(1)}, s32[1,512]{1,0:T(1,128)S(1)}, u32[]{:S(2)}, u32[]{:S(2)}) collective-permute-start(s32[1,512]{1,0:T(1,128)S(1)} %collective-permute-done.4.refs_2_.refs_11_.refs_12_), channel_id=1, source_target_pairs={{0,4},{2,6},{4,12},{6,14},{12,8},{14,10},{8,0},{10,2},{1,5},{3,7},... | collective-permute-start | bytes 6152 | tf_op jit(solution)/shard_map/ppermute | solution.py:204
  46.6 2.3 %collective-permute-done.1.refs_1_.refs_6_ = bf16[256,768]{1,0:T(8,128)(2,1)S(1)} collective-permute-done((bf16[256,768]{1,0:T(8,128)(2,1)}, bf16[256,768]{1,0:T(8,128)(2,1)S(1)}, u32[]{:S(2)}, u32[]{:S(2)}) %collective-permute-start.1) | collective-permute-done | bytes 393248 | tf_op jit(solution)/shard_map/ppermute | solution.py:204
  48.9 0.8 collective-permute-start.13
  49.7 0.0 collective-permute-done.6.refs_5_.refs_4_
  49.7 2.2 %collective-permute-start.2 = (bf16[256,768]{1,0:T(8,128)(2,1)S(1)}, bf16[256,768]{1,0:T(8,128)(2,1)S(1)}, u32[]{:S(2)}, u32[]{:S(2)}) collective-permute-start(bf16[256,768]{1,0:T(8,128)(2,1)S(1)} %collective-permute-done.1.refs_1_.refs_6_), channel_id=1, source_target_pairs={{0,4},{2,6},{4,12},{6,14},{12,8},{14,10},{8,0},{10,2},{1,5},{3,7},... | collective-permute-start | bytes 1179656 | tf_op jit(solution)/shard_map/ppermute | solution.py:204
  51.9 1.1 %shard_map.54 = (f32[1,256]{1,0:T(1,128)S(1)}, f32[1,256]{1,0:T(1,128)S(1)}, f32[1,1024]{1,0:T(1,128)S(1)}) custom-call(s32[2,512]{1,0:T(2,128)S(1)} %broadcast_in_dim.2.refs_0_, bf16[256,768]{1,0:T(8,128)(2,1)S(1)} %copy-done.1, bf16[256,768]{1,0:T(8,128)(2,1)S(1)} %copy-done.3, s32[1,512]{1,0:T(1,128)S(1)} %bitcast.8, s32[1,512]{1,0:T(1,128)S(1)} %bitcast.9, ...), custom_call_target="tpu_custom_call" | custom-call | flops 805306368 | bytes 2359296 | tf_op jit(solution)/shard_map/pallas_call | solution.py:139
  53.1 2.1 %shard_map.55 = (f32[1,256]{1,0:T(1,128)S(1)}, f32[1,1024]{1,0:T(1,128)S(1)}, f32[1,1024]{1,0:T(1,128)S(1)}) custom-call(s32[2,512]{1,0:T(2,128)S(1)} %broadcast_in_dim.2.refs_0_, bf16[256,768]{1,0:T(8,128)(2,1)} %collective-permute-done.11.refs_1_.refs_3_, s32[1,512]{1,0:T(1,128)S(1)} %collective-permute-done.3.refs_2_.refs_7_.refs_8_.refs_9_.refs_10_, ...), custom_call_target="tpu_custom_call" | custom-call | flops 805306368 | bytes 3538944 | tf_op jit(solution)/shard_map/pallas_call | solution.py:139
  55.2 2.1 %shard_map.56 = (f32[1,256]{1,0:T(1,128)S(1)}, f32[1,1024]{1,0:T(1,128)S(1)}, f32[1,1024]{1,0:T(1,128)S(1)}) custom-call(s32[2,512]{1,0:T(2,128)S(1)} %broadcast_in_dim.2.refs_0_, bf16[256,768]{1,0:T(8,128)(2,1)} %collective-permute-done.refs_1_.refs_4_, s32[1,512]{1,0:T(1,128)S(1)} %collective-permute-done.3.refs_2_.refs_7_.refs_8_.refs_9_.refs_10_, ...), custom_call_target="tpu_custom_call" | custom-call | flops 805306368 | bytes 3538944 | tf_op jit(solution)/shard_map/pallas_call | solution.py:139
  57.3 0.0 collective-permute-done.8.refs_10_.refs_6_
  57.3 3.6 %shard_map.57 = (f32[1,256]{1,0:T(1,128)S(1)}, f32[1,256]{1,0:T(1,128)S(1)}, f32[1,256]{1,0:T(1,128)S(1)}, f32[1,256]{1,0:T(1,128)S(1)}, f32[1,512]{1,0:T(1,128)S(1)}, /*index=5*/f32[1,512]{1,0:T(1,128)S(1)}) custom-call(s32[2,512]{1,0:T(2,128)S(1)} %broadcast_in_dim.2.refs_0_, bf16[256,768]{1,0:T(8,128)(2,1)S(1)} %copy-done.1, ...), custom_call_target="tpu_custom_call" | custom-call | flops 1610612736 | bytes 3145728 | tf_op jit(solution)/shard_map/pallas_call | solution.py:139
  60.9 3.0 %shard_map.58 = (f32[1,256]{1,0:T(1,128)S(1)}, f32[1,1024]{1,0:T(1,128)S(1)}, f32[1,1024]{1,0:T(1,128)S(1)}, f32[1,512]{1,0:T(1,128)S(1)}, f32[1,512]{1,0:T(1,128)S(1)}) custom-call(s32[2,512]{1,0:T(2,128)S(1)} %broadcast_in_dim.2.refs_0_, bf16[256,768]{1,0:T(8,128)(2,1)} %collective-permute-done.12.refs_1_.refs_5_, ...), custom_call_target="tpu_custom_call" | custom-call | flops 1207959552 | bytes 5111808 | tf_op jit(solution)/shard_map/pallas_call | solution.py:139
  63.9 2.9 %shard_map.59 = (f32[1,256]{1,0:T(1,128)S(1)}, f32[1,1024]{1,0:T(1,128)S(1)}, f32[1,1024]{1,0:T(1,128)S(1)}, f32[1,512]{1,0:T(1,128)S(1)}, f32[1,512]{1,0:T(1,128)S(1)}) custom-call(s32[2,512]{1,0:T(2,128)S(1)} %broadcast_in_dim.2.refs_0_, bf16[256,768]{1,0:T(8,128)(2,1)S(1)} %collective-permute-done.1.refs_1_.refs_6_, ...), custom_call_target="tpu_custom_call" | custom-call | flops 1207959552 | bytes 5111808 | tf_op jit(solution)/shard_map/pallas_call | solution.py:139
  66.9 0.0 collective-permute-done.10.refs_14_.refs_8_
  66.9 4.3 %shard_map.60 = (f32[1,256]{1,0:T(1,128)S(1)}, f32[1,256]{1,0:T(1,128)S(1)}, f32[1,256]{1,0:T(1,128)S(1)}, f32[1,256]{1,0:T(1,128)S(1)}, f32[1,256]{1,0:T(1,128)...) custom-call(s32[2,512]{1,0:T(2,128)S(1)} %broadcast_in_dim.2.refs_0_, ...), custom_call_target="tpu_custom_call" | custom-call | flops 2415919104 | bytes 3932160 | tf_op jit(solution)/shard_map/pallas_call | solution.py:139
  71.2 3.6 %shard_map.61 = (f32[1,256]{1,0:T(1,128)S(1)}, f32[1,1024]{1,0:T(1,128)S(1)}, f32[1,1024]{1,0:T(1,128)S(1)}, f32[1,512]{1,0:T(1,128)S(1)}, f32[1,512]{1,0:T(1,12...) custom-call(s32[2,512]{1,0:T(2,128)S(1)} %broadcast_in_dim.2.refs_0_, ...), custom_call_target="tpu_custom_call" | custom-call | flops 1610612736 | bytes 6684672 | tf_op jit(solution)/shard_map/pallas_call | solution.py:139
  74.8 3.6 %shard_map.62 = (f32[1,256]{1,0:T(1,128)S(1)}, f32[1,1024]{1,0:T(1,128)S(1)}, f32[1,1024]{1,0:T(1,128)S(1)}, f32[1,512]{1,0:T(1,128)S(1)}, f32[1,512]{1,0:T(1,12...) custom-call(s32[2,512]{1,0:T(2,128)S(1)} %broadcast_in_dim.2.refs_0_, ...), custom_call_target="tpu_custom_call" | custom-call | flops 1610612736 | bytes 6684672 | tf_op jit(solution)/shard_map/pallas_call | solution.py:139
  78.4 0.1 collective-permute-start.18
  78.5 0.1 collective-permute-start.14
  78.6 2.2 %collective-permute-start.17 = (f32[1,512]{1,0:T(1,128)S(1)}, f32[1,512]{1,0:T(1,128)S(1)}, u32[]{:S(2)}, u32[]{:S(2)}) collective-permute-start(f32[1,512]{1,0:T(1,128)S(1)} %pad_maximum_fusion.2), channel_id=1, source_target_pairs={{0,12},{2,14},{4,8},{6,10},{12,0},{14,2},{8,4},{10,6},{1,13},{3,15... | collective-permute-start | bytes 6152 | tf_op jit(solution)/shard_map/ppermute | solution.py:204
  80.8 1.6 %collective-permute-start.15 = (f32[1,1024]{1,0:T(1,128)S(1)}, f32[1,1024]{1,0:T(1,128)S(1)}, u32[]{:S(2)}, u32[]{:S(2)}) collective-permute-start(f32[1,1024]{1,0:T(1,128)S(1)} %slice_add_fusion), channel_id=1, source_target_pairs={{0,2},{2,0},{4,6},{6,4},{8,10},{10,8},{12,14},{14,12},{1,3},{3,1},... | collective-permute-start | bytes 12296 | tf_op jit(solution)/shard_map/ppermute | solution.py:207
  82.4 1.9 %collective-permute-start.16 = (f32[1,512]{1,0:T(1,128)S(1)}, f32[1,512]{1,0:T(1,128)S(1)}, u32[]{:S(2)}, u32[]{:S(2)}) collective-permute-start(f32[1,512]{1,0:T(1,128)S(1)} %pad_maximum_fusion.1), channel_id=1, source_target_pairs={{0,8},{2,10},{4,0},{6,2},{12,4},{14,6},{8,12},{10,14},{1,9},{3,11}... | collective-permute-start | bytes 6152 | tf_op jit(solution)/shard_map/ppermute | solution.py:204
  84.2 1.7 %collective-permute-done.16.refs_5_ = f32[1,512]{1,0:T(1,128)S(1)} collective-permute-done((f32[1,512]{1,0:T(1,128)S(1)}, f32[1,512]{1,0:T(1,128)S(1)}, u32[]{:S(2)}, u32[]{:S(2)}) %collective-permute-start.16) | collective-permute-done | bytes 2080 | tf_op jit(solution)/shard_map/ppermute | solution.py:204
  86.0 0.6 scores.1
  (22 shorter events, 0.1 us)
Async XLA Ops:
  0.6 5.8 %copy-start.4 = (s32[512]{0:T(512)S(1)}, s32[512]{0:T(512)}, u32[]{:S(2)}) copy-start(s32[512]{0:T(512)} %param.5) | copy-start | bytes 6148
  3.2 46.5 %collective-permute-start.6 = (bf16[1024,768]{1,0:T(8,128)(2,1)S(1)}, bf16[1024,768]{1,0:T(8,128)(2,1)S(1)}, u32[]{:S(2)}, u32[]{:S(2)}) collective-permute-start(bf16[1024,768]{1,0:T(8,128)(2,1)S(1)} %get-tuple-element.57.refs_5_.refs_3_), channel_id=1, source_target_pairs={{0,1},{1,0},{2,3},{3,2},{4,5},{5,4},{6,7},{7,6},{8,9},{9,8},{10,11... | collective-permute-start | bytes 4718600 | tf_op jit(solution)/shard_map/ppermute | solution.py:210
  3.8 21.1 %collective-permute-start.7 = (bf16[512,768]{1,0:T(8,128)(2,1)S(1)}, bf16[512,768]{1,0:T(8,128)(2,1)}, u32[]{:S(2)}, u32[]{:S(2)}) collective-permute-start(bf16[512,768]{1,0:T(8,128)(2,1)S(1)} %get-tuple-element.58), channel_id=1, source_target_pairs={{0,2},{2,0},{4,6},{6,4},{8,10},{10,8},{12,14},{14,12},{1,3},{3,1},... | collective-permute-start | bytes 2359304 | tf_op jit(solution)/shard_map/ppermute | solution.py:207
  6.4 35.1 %collective-permute-start.9 = (bf16[512,768]{1,0:T(8,128)(2,1)}, bf16[512,768]{1,0:T(8,128)(2,1)}, u32[]{:S(2)}, u32[]{:S(2)}) collective-permute-start(bf16[512,768]{1,0:T(8,128)(2,1)} %get-tuple-element.59), channel_id=1, source_target_pairs={{0,2},{2,0},{4,6},{6,4},{8,10},{10,8},{12,14},{14,12},{1,3},{3,1},... | collective-permute-start | bytes 2359304 | tf_op jit(solution)/shard_map/ppermute | solution.py:207
  6.4 5.9 %collective-permute-start.3 = (s32[1,512]{1,0:T(1,128)S(1)}, s32[1,512]{1,0:T(1,128)S(1)}, u32[]{:S(2)}, u32[]{:S(2)}) collective-permute-start(s32[1,512]{1,0:T(1,128)S(1)} %bitcast.5), channel_id=1, source_target_pairs={{0,4},{2,6},{4,12},{6,14},{12,8},{14,10},{8,0},{10,2},{1,5},{3,7},... | collective-permute-start | bytes 6152 | tf_op jit(solution)/shard_map/ppermute | solution.py:204
  9.7 17.3 %copy-start = (bf16[256,768]{1,0:T(8,128)(2,1)}, bf16[256,768]{1,0:T(8,128)(2,1)S(1)}, u32[]{:S(2)}) copy-start(bf16[256,768]{1,0:T(8,128)(2,1)S(1)} %shard_map.52.refs_1_) | copy-start | bytes 1179652
  9.7 15.2 %collective-permute-start.11 = (bf16[256,768]{1,0:T(8,128)(2,1)S(1)}, bf16[256,768]{1,0:T(8,128)(2,1)}, u32[]{:S(2)}, u32[]{:S(2)}) collective-permute-start(bf16[256,768]{1,0:T(8,128)(2,1)S(1)} %shard_map.52.refs_1_), channel_id=1, source_target_pairs={{0,4},{2,6},{4,12},{6,14},{12,8},{14,10},{8,0},{10,2},{1,5},{3,7},... | collective-permute-start | bytes 1179656 | tf_op jit(solution)/shard_map/ppermute | solution.py:204
  12.3 9.0 %collective-permute-start.4 = (s32[1,512]{1,0:T(1,128)S(1)}, s32[1,512]{1,0:T(1,128)S(1)}, u32[]{:S(2)}, u32[]{:S(2)}) collective-permute-start(s32[1,512]{1,0:T(1,128)S(1)} %collective-permute-done.3.refs_2_.refs_7_.refs_8_.refs_9_.refs_10_), channel_id=1, source_target_pairs={{0,4},{2,6},{4,12},{6,14},{12,8},{14,10},{8,0},{10,2},{1,5},{3,7},... | collective-permute-start | bytes 6152 | tf_op jit(solution)/shard_map/ppermute | solution.py:204
  21.4 13.0 %collective-permute-start = (bf16[256,768]{1,0:T(8,128)(2,1)S(1)}, bf16[256,768]{1,0:T(8,128)(2,1)}, u32[]{:S(2)}, u32[]{:S(2)}) collective-permute-start(bf16[256,768]{1,0:T(8,128)(2,1)S(1)} %shard_map.50.refs_2_), channel_id=1, source_target_pairs={{0,4},{2,6},{4,12},{6,14},{12,8},{14,10},{8,0},{10,2},{1,5},{3,7},... | collective-permute-start | bytes 1179656 | tf_op jit(solution)/shard_map/ppermute | solution.py:204
  23.1 0.8 copy-start.2
  24.9 32.5 %collective-permute-start.8 = (bf16[512,768]{1,0:T(8,128)(2,1)}, bf16[512,768]{1,0:T(8,128)(2,1)}, u32[]{:S(2)}, u32[]{:S(2)}) collective-permute-start(bf16[512,768]{1,0:T(8,128)(2,1)} %collective-permute-done.7.refs_9_.refs_5_), channel_id=1, source_target_pairs={{0,1},{1,0},{2,3},{3,2},{4,5},{5,4},{6,7},{7,6},{8,9},{9,8},{10,11... | collective-permute-start | bytes 2359304 | tf_op jit(solution)/shard_map/ppermute | solution.py:210
  24.9 19.9 %collective-permute-start.12 = (bf16[256,768]{1,0:T(8,128)(2,1)}, bf16[256,768]{1,0:T(8,128)(2,1)}, u32[]{:S(2)}, u32[]{:S(2)}) collective-permute-start(bf16[256,768]{1,0:T(8,128)(2,1)} %collective-permute-done.11.refs_1_.refs_3_), channel_id=1, source_target_pairs={{0,4},{2,6},{4,12},{6,14},{12,8},{14,10},{8,0},{10,2},{1,5},{3,7},... | collective-permute-start | bytes 1179656 | tf_op jit(solution)/shard_map/ppermute | solution.py:204
  34.4 14.5 %collective-permute-start.1 = (bf16[256,768]{1,0:T(8,128)(2,1)}, bf16[256,768]{1,0:T(8,128)(2,1)S(1)}, u32[]{:S(2)}, u32[]{:S(2)}) collective-permute-start(bf16[256,768]{1,0:T(8,128)(2,1)} %collective-permute-done.refs_1_.refs_4_), channel_id=1, source_target_pairs={{0,4},{2,6},{4,12},{6,14},{12,8},{14,10},{8,0},{10,2},{1,5},{3,7},... | collective-permute-start | bytes 1179656 | tf_op jit(solution)/shard_map/ppermute | solution.py:204
  41.4 25.4 %collective-permute-start.10 = (bf16[512,768]{1,0:T(8,128)(2,1)}, bf16[512,768]{1,0:T(8,128)(2,1)S(1)}, u32[]{:S(2)}, u32[]{:S(2)}) collective-permute-start(bf16[512,768]{1,0:T(8,128)(2,1)} %collective-permute-done.9.refs_13_.refs_7_), channel_id=1, source_target_pairs={{0,1},{1,0},{2,3},{3,2},{4,5},{5,4},{6,7},{7,6},{8,9},{9,8},{10,11... | collective-permute-start | bytes 2359304 | tf_op jit(solution)/shard_map/ppermute | solution.py:210
  41.6 1.0 %copy-start.1 = (bf16[256,768]{1,0:T(8,128)(2,1)S(1)}, bf16[256,768]{1,0:T(8,128)(2,1)}, u32[]{:S(2)}) copy-start(bf16[256,768]{1,0:T(8,128)(2,1)} %copy-done) | copy-start | bytes 1179652
  42.6 1.0 %copy-start.3 = (bf16[256,768]{1,0:T(8,128)(2,1)S(1)}, bf16[256,768]{1,0:T(8,128)(2,1)}, u32[]{:S(2)}) copy-start(bf16[256,768]{1,0:T(8,128)(2,1)} %copy-done.2) | copy-start | bytes 1179652
  44.7 26.4 %collective-permute-start.5 = (s32[1,512]{1,0:T(1,128)S(1)}, s32[1,512]{1,0:T(1,128)S(1)}, u32[]{:S(2)}, u32[]{:S(2)}) collective-permute-start(s32[1,512]{1,0:T(1,128)S(1)} %collective-permute-done.4.refs_2_.refs_11_.refs_12_), channel_id=1, source_target_pairs={{0,4},{2,6},{4,12},{6,14},{12,8},{14,10},{8,0},{10,2},{1,5},{3,7},... | collective-permute-start | bytes 6152 | tf_op jit(solution)/shard_map/ppermute | solution.py:204
  48.9 22.3 %collective-permute-start.13 = (bf16[256,768]{1,0:T(8,128)(2,1)}, bf16[256,768]{1,0:T(8,128)(2,1)S(1)}, u32[]{:S(2)}, u32[]{:S(2)}) collective-permute-start(bf16[256,768]{1,0:T(8,128)(2,1)} %collective-permute-done.12.refs_1_.refs_5_), channel_id=1, source_target_pairs={{0,4},{2,6},{4,12},{6,14},{12,8},{14,10},{8,0},{10,2},{1,5},{3,7},... | collective-permute-start | bytes 1179656 | tf_op jit(solution)/shard_map/ppermute | solution.py:204
  49.7 25.1 %collective-permute-start.2 = (bf16[256,768]{1,0:T(8,128)(2,1)S(1)}, bf16[256,768]{1,0:T(8,128)(2,1)S(1)}, u32[]{:S(2)}, u32[]{:S(2)}) collective-permute-start(bf16[256,768]{1,0:T(8,128)(2,1)S(1)} %collective-permute-done.1.refs_1_.refs_6_), channel_id=1, source_target_pairs={{0,4},{2,6},{4,12},{6,14},{12,8},{14,10},{8,0},{10,2},{1,5},{3,7},... | collective-permute-start | bytes 1179656 | tf_op jit(solution)/shard_map/ppermute | solution.py:204
  78.4 5.8 %collective-permute-start.18 = (f32[1,512]{1,0:T(1,128)S(1)}, f32[1,512]{1,0:T(1,128)S(1)}, u32[]{:S(2)}, u32[]{:S(2)}) collective-permute-start(f32[1,512]{1,0:T(1,128)S(1)} %pad_maximum_fusion.3), channel_id=1, source_target_pairs={{0,4},{2,6},{4,12},{6,14},{12,8},{14,10},{8,0},{10,2},{1,5},{3,7},... | collective-permute-start | bytes 6152 | tf_op jit(solution)/shard_map/ppermute | solution.py:204
  78.5 2.3 %collective-permute-start.14 = (f32[1,2048]{1,0:T(1,128)S(1)}, f32[1,2048]{1,0:T(1,128)S(1)}, u32[]{:S(2)}, u32[]{:S(2)}) collective-permute-start(f32[1,2048]{1,0:T(1,128)S(1)} %pad_maximum_fusion), channel_id=1, source_target_pairs={{0,1},{1,0},{2,3},{3,2},{4,5},{5,4},{6,7},{7,6},{8,9},{9,8},{10,11... | collective-permute-start | bytes 24584 | tf_op jit(solution)/shard_map/ppermute | solution.py:210
  78.6 5.7 %collective-permute-start.17 = (f32[1,512]{1,0:T(1,128)S(1)}, f32[1,512]{1,0:T(1,128)S(1)}, u32[]{:S(2)}, u32[]{:S(2)}) collective-permute-start(f32[1,512]{1,0:T(1,128)S(1)} %pad_maximum_fusion.2), channel_id=1, source_target_pairs={{0,12},{2,14},{4,8},{6,10},{12,0},{14,2},{8,4},{10,6},{1,13},{3,15... | collective-permute-start | bytes 6152 | tf_op jit(solution)/shard_map/ppermute | solution.py:204
  80.8 5.2 %collective-permute-start.15 = (f32[1,1024]{1,0:T(1,128)S(1)}, f32[1,1024]{1,0:T(1,128)S(1)}, u32[]{:S(2)}, u32[]{:S(2)}) collective-permute-start(f32[1,1024]{1,0:T(1,128)S(1)} %slice_add_fusion), channel_id=1, source_target_pairs={{0,2},{2,0},{4,6},{6,4},{8,10},{10,8},{12,14},{14,12},{1,3},{3,1},... | collective-permute-start | bytes 12296 | tf_op jit(solution)/shard_map/ppermute | solution.py:207
  82.4 3.6 %collective-permute-start.16 = (f32[1,512]{1,0:T(1,128)S(1)}, f32[1,512]{1,0:T(1,128)S(1)}, u32[]{:S(2)}, u32[]{:S(2)}) collective-permute-start(f32[1,512]{1,0:T(1,128)S(1)} %pad_maximum_fusion.1), channel_id=1, source_target_pairs={{0,8},{2,10},{4,0},{6,2},{12,4},{14,6},{8,12},{10,14},{1,9},{3,11}... | collective-permute-start | bytes 6152 | tf_op jit(solution)/shard_map/ppermute | solution.py:204
